TPU v7x, 512 devices: a 8x2x16 block of a 8x8x16 slice. The times are simulated.
512 devices in a mesh: groups: 2 (over y), docs: 16 (over z), mp: 8 (over x), sub: 2 (over core).
Axes of the slice: x: 8, y: 2, z: 16, core: 2. Of those that a mesh axis runs over, the one named last changes fastest.
The devices are a block of a 8x8x16 slice.
Arguments:
- embeddings: bfloat16 [65536, 1024], P(('groups', 'docs', 'mp', 'sub')), parts along dimension 0, may hold values from -6 to 6
- owner_shard: int32 [65536, 1], P(('groups', 'docs', 'mp', 'sub')), parts along dimension 0, may hold values from 0 to 15; in each aligned block of 128 rows (0 to 127, 128 to 255, ...) at most 16 rows name the same one
- query_local: int32 [65536], P(('groups', 'docs', 'mp', 'sub')), parts along dimension 0, may hold values from 0 to 1
- labels: int32 [65536], P(('groups', 'docs', 'mp', 'sub')), parts along dimension 0, may hold values from 0 to 4
- w_first: bfloat16 [1024, 1024], replicated, may hold values from -0.1875 to 0.1875
- w_second: float32 [1024], replicated, may hold values from -0.1875 to 0.1875
Outputs:
- emb_grad: bfloat16 [65536, 1024], P(('groups', 'docs', 'mp', 'sub')), parts along dimension 0
- w_first_grad: float32 [2048, 1024], P(('groups', 'mp', 'sub')), parts along dimension 0
- w_second_grad: float32 [2048], P('groups'), parts along dimension 0
There are 2 independent parts, one for each index of `groups`. A program takes and returns all parts, laid end to end along the dimension named above; an argument that names none is the same for every part. Nothing has to cross between parts.
Inputs may be any that keep to these rules, and one draw needn't show every extreme that they name: `owner_shard`: among the 128 rows of one document shard no owner appears more than 16 times, and some owner appears exactly 16 times.
All inputs are finite; a program needn't handle non-finite values.
Results may differ from a plain program's by a relative error of at most 0.017.
Values may be sent and summed in bfloat16 or wider, within the bound.
A program may use at most 64 MiB of HBM per device.

v0:
```python
import functools
import math

import jax
import jax.numpy as jnp
from jax import lax
from jax.sharding import PartitionSpec as P

Q_DEV = 2


ranking_softness = 1.0


def one_axis_at_a_time(x, axes):
    return functools.reduce(lax.psum, axes, x)


def split_up(x, dim, count):
    before, after = (x.shape[:dim], x.shape[dim + 1 :])
    return jnp.moveaxis(x.reshape(*before, count, -1, *after), dim, 0)


def summed_on_arrival(x, axis, dim):
    tiles = split_up(x, dim, lax.axis_size(axis))
    arrived = lax.all_to_all(tiles, axis, split_axis=0, concat_axis=0, tiled=True)
    return arrived.astype(jnp.float32).sum(axis=0)


def sent_to_all(x, axis):
    count = lax.axis_size(axis)
    return lax.all_to_all(jnp.broadcast_to(x[None], (count, *x.shape)), axis, 0, 0, tiled=True)


def of_everyone(x, axis):
    return sent_to_all(x, axis).astype(jnp.float32).sum(axis=0)


def silu_slope(pre_act):
    sigmoid_v = jax.nn.sigmoid(pre_act)
    return sigmoid_v * (1.0 + pre_act * (1.0 - sigmoid_v))


def rank_rows(row_start, row_count, scorer_outputs, query_mark, grade_slot):
    slot_index = jnp.arange(scorer_outputs.shape[0], dtype=jnp.int32)
    row_index = row_start + jnp.arange(row_count, dtype=jnp.int32)
    matching_query = (query_mark[:, None] == query_mark[None, :]) & (query_mark[:, None] > 0)
    smooth_rank = (
        jnp.sum(
            jnp.where(
                matching_query,
                jax.nn.sigmoid(
                    (scorer_outputs[None, :] - scorer_outputs[:, None]) / ranking_softness
                ),
                0.0,
            ),
            axis=1,
        )
        - 0.5
    )
    higher = (grade_slot[None, :] > grade_slot[:, None]) | (
        grade_slot[None, :] == grade_slot[:, None]
    ) & (slot_index[None, :] < row_index[:, None])
    ideal_rank = jnp.sum((matching_query & higher).astype(jnp.float32), axis=1)
    row_gain = jnp.exp2(grade_slot.astype(jnp.float32)) - 1.0
    return (smooth_rank, row_gain / jnp.log2(2.0 + ideal_rank))


def lambda_rows(scorer_outputs, query_mark, grade_slot, discount, inv_ideal):
    gain_all = jnp.exp2(grade_slot.astype(jnp.float32)) - 1.0
    matching_query = (query_mark[:, None] == query_mark[None, :]) & (query_mark[:, None] > 0)
    score_gap = scorer_outputs[:, None] - scorer_outputs[None, :]
    weights = (
        jnp.abs(gain_all[:, None] - gain_all[None, :])
        * jnp.abs(discount[:, None] - discount[None, :])
        * inv_ideal[:, None]
    )
    direction = jnp.where(
        grade_slot[:, None] > grade_slot[None, :], -jax.nn.sigmoid(-score_gap), 0.0
    ) + jnp.where(grade_slot[None, :] > grade_slot[:, None], jax.nn.sigmoid(score_gap), 0.0)
    return jnp.sum(jnp.where(matching_query, weights * direction, 0.0), axis=1)


def owner_lambdas(scorer_outputs, query_mark, grade_slot):
    slot_total = scorer_outputs.shape[0]
    row_count = math.gcd(slot_total, 512)
    starts = jnp.arange(0, slot_total, row_count, dtype=jnp.int32)

    def rank_block(first_row):
        return rank_rows(first_row, row_count, scorer_outputs, query_mark, grade_slot)

    smooth_rank, ideal_term = lax.map(rank_block, starts)
    smooth_rank = smooth_rank.reshape(slot_total)
    ideal_term = ideal_term.reshape(slot_total)
    discount = 1.0 / jnp.log2(2.0 + smooth_rank)
    member = (query_mark[:, None] == jnp.arange(1, Q_DEV + 1, dtype=jnp.int32)[None, :]).astype(
        jnp.float32
    )
    per_query = jnp.dot(ideal_term, member, precision=lax.Precision.HIGHEST)
    idcg = jnp.dot(member, per_query, precision=lax.Precision.HIGHEST)
    inv_ideal = jnp.where(idcg > 0.0, 1.0 / jnp.where(idcg > 0.0, idcg, 1.0), 0.0)

    def lambda_block(first_row):
        return lambda_rows(scorer_outputs, query_mark, grade_slot, discount, inv_ideal)

    return lax.map(lambda_block, starts).reshape(slot_total)


def column_product(source, pre_grad):
    return lax.dot_general(
        source, pre_grad, (((0,), (0,)), ((), ())), preferred_element_type=jnp.float32
    )


def weight_grads(inputs, pre_grad, hidden, lambdas):
    second_part = jnp.dot(lambdas, hidden, precision=lax.Precision.HIGHEST)
    second_grad = one_axis_at_a_time(second_part, ("docs", "mp", "sub"))
    lane_part = summed_on_arrival(
        column_product(inputs, pre_grad).astype(jnp.bfloat16), ("mp", "sub"), 0
    )
    first_grad = of_everyone(lane_part.astype(jnp.bfloat16), "docs").astype(jnp.float32)
    return (first_grad, second_grad)


def on_device(embeddings, owner_shard, query_local, labels, w_first, w_second):
    doc_count = lax.axis_size("docs")
    resident_rows = embeddings.shape[0]
    capacity = 2 * resident_rows // doc_count
    slot_count = doc_count * capacity
    target = owner_shard[:, 0]
    owner_hit = (target[:, None] == jnp.arange(doc_count, dtype=jnp.int32)[None, :]).astype(
        jnp.int32
    )
    earlier = jnp.cumsum(owner_hit, axis=0) - owner_hit
    slot_of = target * capacity + jnp.sum(earlier * owner_hit, axis=1)
    query_mark = jnp.zeros((slot_count,), jnp.int32).at[slot_of].set(query_local + 1)
    grade_slot = jnp.zeros((slot_count,), jnp.int32).at[slot_of].set(labels)
    row_info = jnp.stack(
        [query_mark.reshape(doc_count, capacity), grade_slot.reshape(doc_count, capacity)], axis=1
    )
    pre_act = jnp.dot(embeddings, w_first, preferred_element_type=jnp.float32)
    hidden = pre_act * jax.nn.sigmoid(pre_act)
    own_scores = jnp.dot(hidden, w_second, precision=lax.Precision.HIGHEST)
    outgoing = (
        jnp.zeros((slot_count,), jnp.float32)
        .at[slot_of]
        .set(own_scores)
        .reshape(doc_count, capacity)
    )
    incoming, info_in = (
        lax.all_to_all(outgoing, "docs", split_axis=0, concat_axis=0, tiled=True),
        lax.all_to_all(row_info, "docs", split_axis=0, concat_axis=0, tiled=True),
    )
    slot_lambdas = owner_lambdas(
        incoming.reshape(slot_count),
        info_in[:, 0, :].reshape(slot_count),
        info_in[:, 1, :].reshape(slot_count),
    )
    gathered_back = lax.all_to_all(
        slot_lambdas.reshape(doc_count, capacity), "docs", split_axis=0, concat_axis=0, tiled=True
    )
    lambdas = gathered_back.reshape(slot_count)[slot_of]
    pre_grad = (lambdas[:, None] * w_second[None, :] * silu_slope(pre_act)).astype(jnp.bfloat16)
    emb_grad = lax.dot_general(
        pre_grad, w_first, (((1,), (1,)), ((), ())), preferred_element_type=jnp.float32
    ).astype(jnp.bfloat16)
    w_first_grad, w_second_grad = weight_grads(embeddings, pre_grad, hidden, lambdas)
    return (emb_grad, w_first_grad, w_second_grad)


def solution(mesh):
    return jax.shard_map(
        on_device,
        mesh=mesh,
        in_specs=(
            P(("groups", "docs", "mp", "sub"), None),
            P(("groups", "docs", "mp", "sub"), None),
            P(("groups", "docs", "mp", "sub")),
            P(("groups", "docs", "mp", "sub")),
            P(),
            P(),
        ),
        out_specs=(
            P(("groups", "docs", "mp", "sub"), None),
            P(("groups", "mp", "sub"), None),
            P("groups"),
        ),
        check_vma=False,
    )
```

profile of v0, /device:TPU:65, one launch (start us, length us, event | category | flops | bytes accessed | tf_op | source)
XLA Modules:
  0.0 305.1 jit_solution(15351514070500478508)
XLA Ops:
  0.6 0.0 copy-start
  0.6 0.0 copy-start.2
  0.7 0.9 fusion.22
  1.5 0.2 reduce_window_sum.11
  1.7 0.8 select_reduce_fusion.1
  2.5 0.7 fusion.25
  3.2 1.4 fusion.35
  4.6 0.0 copy-start.1
  4.7 0.6 convolution_bitcast_fusion.1
  5.3 1.0 scatter_custom_fusion.2
  6.3 0.7 all_to_all.22
  6.9 44.2 %all-to-all-start.1 = ((f32[16,1,16]{2,1,0:T(1,128)}), f32[16,1,16]{2,1,0:T(1,128)S(1)}, u32[]{:S(2)}, u32[]{:S(2)}) async-start(f32[16,1,16]{2,1,0:T(1,128)} %all_to_all.22), calls=%async_computation.1 | async-start | bytes 16384 | tf_op jit(solution)/shard_map/all_to_all | solution.py:151
  51.2 1.0 scatter_custom_fusion
  52.2 1.1 scatter_custom_fusion.1
  53.3 0.1 stack_reshape.7
  53.4 0.1 stack_reshape.6
  53.5 0.6 pad_add_fusion
  54.1 8.1 %all-to-all-done.1 = f32[16,1,16]{2,1,0:T(1,128)S(1)} async-done(((f32[16,1,16]{2,1,0:T(1,128)}), f32[16,1,16]{2,1,0:T(1,128)S(1)}, u32[]{:S(2)}, u32[]{:S(2)}) %all-to-all-start.1) | async-done | bytes 1056 | tf_op jit(solution)/shard_map/all_to_all | solution.py:151
  62.2 3.9 %all-to-all-start = ((s32[16,2,16]{2,1,0:T(2,128)}), s32[16,2,16]{2,1,0:T(2,128)S(1)}, u32[]{:S(2)}, u32[]{:S(2)}) async-start(s32[16,2,16]{2,1,0:T(2,128)} %pad_add_fusion), calls=%async_computation | async-start | bytes 32768 | tf_op jit(solution)/shard_map/all_to_all | solution.py:152
  66.2 0.5 broadcast.187
  66.7 0.7 reduce.15
  67.4 0.1 sub.97
  67.4 9.7 %all-to-all-done = s32[16,2,16]{2,1,0:T(2,128)S(1)} async-done(((s32[16,2,16]{2,1,0:T(2,128)}), s32[16,2,16]{2,1,0:T(2,128)S(1)}, u32[]{:S(2)}, u32[]{:S(2)}) %all-to-all-start) | async-done | bytes 2080 | tf_op jit(solution)/shard_map/all_to_all | solution.py:152
  77.2 0.1 eq.78
  77.3 0.1 reshape_squeeze.3
  77.4 0.3 select_reduce_fusion
  77.7 0.2 convolution_bitcast_fusion
  78.0 0.2 fusion.14
  78.2 0.4 fusion.4
  78.6 0.7 all_to_all.24
  79.3 3.9 %all-to-all-start.2 = ((f32[16,1,16]{2,1,0:T(1,128)}), f32[16,1,16]{2,1,0:T(1,128)S(1)}, u32[]{:S(2)}, u32[]{:S(2)}) async-start(f32[16,1,16]{2,1,0:T(1,128)} %all_to_all.24), calls=%async_computation.2 | async-start | bytes 16384 | tf_op jit(solution)/shard_map/all_to_all | solution.py:159
  83.3 10.8 %all-to-all-done.2 = f32[16,1,16]{2,1,0:T(1,128)S(1)} async-done(((f32[16,1,16]{2,1,0:T(1,128)}), f32[16,1,16]{2,1,0:T(1,128)S(1)}, u32[]{:S(2)}, u32[]{:S(2)}) %all-to-all-start.2) | async-done | bytes 1056 | tf_op jit(solution)/shard_map/all_to_all | solution.py:159
  94.1 0.7 reduce.16
  94.7 0.1 reshape.81
  94.8 1.3 gather_fusion
  96.1 0.0 copy-done.1
  96.1 0.8 convolution_convert_fusion
  96.9 62.4 %all_to_all.33 = bf16[16,64,1024]{2,1,0:T(8,128)(2,1)} all-to-all(bf16[16,64,1024]{2,1,0:T(8,128)(2,1)S(1)} %bitcast.32), channel_id=1, replica_groups=mesh['groups'=2,'docs'=16,'mp'=8,'sub'=2] {'mp','sub'}, dimensions={0} | all-to-all | bytes 4194304 | tf_op jit(solution)/shard_map/all_to_all | solution.py:26
  159.3 2.0 reduce_sum.67
  161.3 1.6 broadcast_in_dim.48
  162.9 4.8 %all-to-all-start.4 = ((bf16[16,64,1024]{2,1,0:T(8,128)(2,1)}), bf16[16,64,1024]{2,1,0:T(8,128)(2,1)}, u32[]{:S(2)}, u32[]{:S(2)}) async-start(bf16[16,64,1024]{2,1,0:T(8,128)(2,1)} %broadcast_in_dim.48), calls=%async_computation.4 | async-start | bytes 4194304 | tf_op jit(solution)/shard_map/all_to_all | solution.py:32
  167.7 0.5 fusion.17
  168.2 109.1 %psum.21 = f32[1024]{0:T(1024)S(1)} all-reduce(f32[1024]{0:T(1024)S(1)} %bitcast.33), channel_id=1, replica_groups=mesh['groups'=2,'docs'=16,'mp'=8,'sub'=2] {'docs'}, use_global_device_ids=true, to_apply=%region_10.11 | all-reduce | flops 1024 | bytes 8192 | tf_op jit(solution)/shard_map/psum | solution.py:16
  277.3 10.8 %psum.22 = f32[1024]{0:T(1024)S(1)} all-reduce(f32[1024]{0:T(1024)S(1)} %psum.21), channel_id=1, replica_groups=mesh['groups'=2,'docs'=16,'mp'=8,'sub'=2] {'mp'}, use_global_device_ids=true, to_apply=%region_11.12 | all-reduce | flops 1024 | bytes 8192 | tf_op jit(solution)/shard_map/psum | solution.py:16
  288.0 12.8 %psum.23 = f32[1024]{0:T(1024)} all-reduce(f32[1024]{0:T(1024)S(1)} %psum.22), channel_id=1, replica_groups=mesh['groups'=2,'docs'=16,'mp'=8,'sub'=2] {'sub'}, use_global_device_ids=true, to_apply=%region_12.13 | all-reduce | flops 1024 | bytes 8192 | tf_op jit(solution)/shard_map/psum | solution.py:16
  300.8 1.5 convolution_convert_fusion.1
  302.4 0.0 all-to-all-done.4
  302.4 2.7 convert_reduce_fusion
  (11 shorter events, 0.1 us)
Async XLA Ops:
  0.6 2.6 copy-start
  0.6 4.0 %copy-start.2 = (f32[1024]{0:T(1024)S(1)}, f32[1024]{0:T(1024)}, u32[]{:S(2)}) copy-start(f32[1024]{0:T(1024)} %param.11) | copy-start | bytes 12292
  3.2 48.0 %copy-start.3 = (s32[128]{0:T(128)S(1)}, s32[128]{0:T(128)}, u32[]{:S(2)}) copy-start(s32[128]{0:T(128)} %param.8) | copy-start | bytes 1540
  4.6 91.5 %copy-start.1 = (bf16[128,1024]{1,0:T(8,128)(2,1)S(1)}, bf16[128,1024]{1,0:T(8,128)(2,1)}, u32[]{:S(2)}) copy-start(bf16[128,1024]{1,0:T(8,128)(2,1)} %param.6) | copy-start | bytes 786436
  6.9 55.3 %all-to-all-start.1 = ((f32[16,1,16]{2,1,0:T(1,128)}), f32[16,1,16]{2,1,0:T(1,128)S(1)}, u32[]{:S(2)}, u32[]{:S(2)}) async-start(f32[16,1,16]{2,1,0:T(1,128)} %all_to_all.22), calls=%async_computation.1 | async-start | bytes 16384 | tf_op jit(solution)/shard_map/all_to_all | solution.py:151
  62.2 14.9 %all-to-all-start = ((s32[16,2,16]{2,1,0:T(2,128)}), s32[16,2,16]{2,1,0:T(2,128)S(1)}, u32[]{:S(2)}, u32[]{:S(2)}) async-start(s32[16,2,16]{2,1,0:T(2,128)} %pad_add_fusion), calls=%async_computation | async-start | bytes 32768 | tf_op jit(solution)/shard_map/all_to_all | solution.py:152
  79.3 14.7 %all-to-all-start.2 = ((f32[16,1,16]{2,1,0:T(1,128)}), f32[16,1,16]{2,1,0:T(1,128)S(1)}, u32[]{:S(2)}, u32[]{:S(2)}) async-start(f32[16,1,16]{2,1,0:T(1,128)} %all_to_all.24), calls=%async_computation.2 | async-start | bytes 16384 | tf_op jit(solution)/shard_map/all_to_all | solution.py:159
  162.9 139.5 %all-to-all-start.4 = ((bf16[16,64,1024]{2,1,0:T(8,128)(2,1)}), bf16[16,64,1024]{2,1,0:T(8,128)(2,1)}, u32[]{:S(2)}, u32[]{:S(2)}) async-start(bf16[16,64,1024]{2,1,0:T(8,128)(2,1)} %broadcast_in_dim.48), calls=%async_computation.4 | async-start | bytes 4194304 | tf_op jit(solution)/shard_map/all_to_all | solution.py:32
where the time goes:
time: 306 us; the launch traced here: 305 us
  blocking collectives  195 us (64%)
  starting transfers between devices  56.9 us (19%)
  waiting for transfers between devices  28.6 us (9%)
  other arithmetic  10 us (3%)
  local copies, waits for them, and re-layouts  8.37 us (3%)
  matrix products  5.27 us (2%)
    psum x3, blocking collectives, one_axis_at_a_time(): return functools.reduce(lax.psum, axes, x)  133 us
    all_to_all x1, blocking collectives, summed_on_arrival(): lax.all_to_all(tiles, axis, split_axis=0, concat_axis=0, tiled=True)  62.4 us
    all_to_all x1, starting transfers between devices, on_device(): lax.all_to_all(outgoing, 'docs', split_axis=0, concat_axis=0, tiled=True)  44.2 us
    all_to_all x1, waiting for transfers between devices, on_device(): lax.all_to_all(slot_lambdas.reshape(doc_count, capacity), 'docs', split_a...  10.8 us
    all_to_all x1, waiting for transfers between devices, on_device(): lax.all_to_all(row_info, 'docs', split_axis=0, concat_axis=0, tiled=True)  9.69 us
    all_to_all x1, waiting for transfers between devices, on_device(): lax.all_to_all(outgoing, 'docs', split_axis=0, concat_axis=0, tiled=True)  8.12 us
  transfers between devices with their start and end apart: 4, of which 3 were waited for; matrix products, arithmetic and copies ran while one was open for 2% of the time, Pallas kernels for 0%

commit v1 on v0

v1 whole, which is shorter than its diff:
```python
import functools
import math

import jax
import jax.numpy as jnp
from jax import lax
from jax.experimental import pallas as pl
from jax.experimental.pallas import tpu as pltpu
from jax.sharding import PartitionSpec as P

MESH = pl.DeviceIdType.MESH
F32 = jnp.float32
BF16 = jnp.bfloat16

NQ = 4
LN2 = math.log(2.0)
FWD = 4


def remote(src, dst, send_sem, recv_sem, where):
    return pltpu.make_async_remote_copy(
        src_ref=src, dst_ref=dst, send_sem=send_sem, recv_sem=recv_sem, device_id=where, device_id_type=MESH
    )


def by_distance(count):
    return sorted(range(1, count), key=lambda k: -min(k, count - k))


def step_kernel(
    nd, nm, rows, width, cap,
    emb_h, own_h, qry_h, lab_h, w1_h, w2_h,
    eg_h, wg_h, w2g_h,
    emb_v, own_v, qry_v, lab_v, w1_v, w2_v,
    slope_v, hid_v, hit_v,
    meta_s, meta_r, score_s, score_r,
    sa, sm, sg, sd, disc_v,
    embp_v, emb_t, pg, pg_in, g_v,
    x_s, x_r, z_s, z_r, z_f, ag_r, out_v, eg_v,
    w2_own, w2_x, w2_sum, w2_in, w2_z, w2_out,
    load_sem, out_sem, meta_ss, meta_rs, score_ss, score_rs,
    pair_ss, pair_rs, x_ss, x_rs, z_ss, z_rs, ag_ss, ag_rs,
    w2x_ss, w2x_rs, w2z_ss, w2z_rs,
):
    d = lax.axis_index("docs")
    m = lax.axis_index("mp")
    s = lax.axis_index("sub")
    other = 1 - s
    slots = nd * cap
    half = width // 2
    piece = half // NQ

    barrier = pltpu.get_barrier_semaphore()
    for k in by_distance(nd):
        for core in (s, other):
            pl.semaphore_signal(barrier, inc=1, device_id={"docs": lax.rem(d + k, nd), "sub": core}, device_id_type=MESH)
    for k in by_distance(nm):
        pl.semaphore_signal(barrier, inc=1, device_id={"mp": lax.rem(m + k, nm)}, device_id_type=MESH)
    pl.semaphore_signal(barrier, inc=1, device_id={"sub": other}, device_id_type=MESH)

    loads = [
        pltpu.make_async_copy(a, b, load_sem.at[i])
        for i, (a, b) in enumerate(
            ((own_h, own_v), (qry_h, qry_v), (lab_h, lab_v), (w2_h, w2_v), (emb_h, emb_v))
        )
    ]
    cols = width // FWD
    w_loads = [
        pltpu.make_async_copy(
            w1_h.at[:, pl.ds(i * cols, cols)], w1_v.at[:, pl.ds(i * cols, cols)], load_sem.at[5 + i]
        )
        for i in range(FWD)
    ]
    for copy in loads + w_loads:
        copy.start()

    for copy in loads[:3]:
        copy.wait()
    row_i = lax.broadcasted_iota(jnp.int32, (rows, rows), 0)
    col_i = lax.broadcasted_iota(jnp.int32, (rows, rows), 1)
    eye = row_i == col_i

    def upright(row):
        return jnp.sum(jnp.where(eye, row, 0.0), axis=1, keepdims=True)

    own_row = own_v[...].astype(F32)
    own_col = upright(own_row)
    earlier = jnp.sum(
        jnp.where((own_col == own_row) & (col_i < row_i), 1.0, 0.0), axis=1, keepdims=True
    )
    slot_col = own_col * cap + earlier
    hit = slot_col == lax.broadcasted_iota(jnp.int32, (rows, slots), 1).astype(F32)
    hit_v[...] = jnp.where(hit, 1.0, 0.0)

    def slotted(col):
        return jnp.sum(jnp.where(hit_v[...] > 0.0, col, 0.0), axis=0, keepdims=True)

    mark_own = slotted(upright(qry_v[...].astype(F32)) + 1.0)
    label_own = slotted(upright(lab_v[...].astype(F32)))
    meta_s[0:1, :] = mark_own.astype(BF16)
    meta_s[1:2, :] = label_own.astype(BF16)
    meta_r[d, 0:1, :] = mark_own.astype(BF16)
    meta_r[d, 1:2, :] = label_own.astype(BF16)

    for copy in loads[3:]:
        copy.wait()
    score = jnp.zeros((rows, 1), F32)
    for i in range(FWD):
        w_loads[i].wait()
        at = pl.ds(i * cols, cols)
        pre = jnp.dot(emb_v[...], w1_v[:, at], preferred_element_type=F32)
        sig = 0.5 + 0.5 * jnp.tanh(0.5 * pre)
        hid = pre * sig
        w2 = w2_v[:, at]
        hid_v[:, at] = hid
        score += jnp.sum(hid * w2, axis=1, keepdims=True)
        slope_v[:, at] = w2 * (sig * (1.0 + pre * (1.0 - sig)))
    score_own = slotted(0.5 * score)
    score_s[...] = score_own
    score_r[d] = score_own

    pl.semaphore_wait(barrier, 2 * (nd - 1) + (nm - 1) + 1)

    score_sends, meta_sends = [], []
    for k in by_distance(nd):
        where = {"docs": lax.rem(d + k, nd)}
        meta_sends.append(remote(meta_s, meta_r.at[d], meta_ss.at[k], meta_rs.at[d], where))
        meta_sends[-1].start()
        score_sends.append(remote(score_s, score_r.at[d], score_ss.at[k], score_rs.at[d], where))
        score_sends[-1].start()
    emb_send = remote(emb_v, embp_v, pair_ss.at[0], pair_rs.at[0], {"sub": other})
    emb_send.start()

    def turn(block, at):
        for c in range(nm):
            w = width // nm
            emb_t[c, :, at * rows : (at + 1) * rows] = (
                block[:, c * w : (c + 1) * w].astype(F32).T.astype(BF16)
            )

    turn(emb_v, 0)
    emb_send.wait_recv()
    turn(embp_v, 1)

    for k in by_distance(nd):
        src = lax.rem(d + k, nd)
        remote(meta_s, meta_r.at[src], meta_ss.at[k], meta_rs.at[src], {"docs": src}).wait_recv()
    lane = lax.broadcasted_iota(jnp.int32, (nd, slots), 1)
    in_group = lax.rem(lane, cap)

    def turned(a, by):
        near = pltpu.roll(a, by, 1)
        far = pltpu.roll(a, by + slots - cap, 1)
        return jnp.where(in_group >= by, near, far)

    mark = jnp.concatenate([meta_r[i, 0:1, :].astype(F32) for i in range(nd)], axis=0)
    label = jnp.concatenate([meta_r[i, 1:2, :].astype(F32) for i in range(nd)], axis=0)
    gain = jnp.exp2(label) - 1.0
    sm[0] = mark
    sg[0] = gain

    for by in range(1, cap):
        sm[by] = turned(mark, by)
        sg[by] = turned(gain, by)

    group_r = lax.broadcasted_iota(jnp.int32, (slots, slots), 0) // cap
    group_c = lax.broadcasted_iota(jnp.int32, (slots, slots), 1) // cap
    groups = jnp.where(group_r == group_c, 1.0, 0.0).astype(BF16)
    tallies = []
    for q in (1.0, 2.0):
        for least in range(5):
            tallies.append(
                jnp.sum(jnp.where((mark == q) & (label >= float(least)), 1.0, 0.0), axis=0, keepdims=True)
            )
    tallies += [jnp.zeros((6, slots), F32)]
    counts = jnp.dot(jnp.concatenate(tallies, axis=0).astype(BF16), groups, preferred_element_type=F32)
    total = jnp.where(mark == 1.0, counts[0:1], counts[5:6])
    at_least = jnp.where(mark_own == 1.0, counts[1:5], counts[6:10])

    def rank_weight(r, acc):
        r = r.astype(F32)
        w = LN2 / jnp.log(jnp.full((4, slots), 2.0, F32) + r)
        return acc + jnp.where(at_least > r, w, 0.0)

    ladder = lax.fori_loop(0, slots, rank_weight, jnp.zeros((4, slots), F32), unroll=8)
    idcg = ladder[0:1] + 2.0 * ladder[1:2] + 4.0 * ladder[2:3] + 8.0 * ladder[3:4]
    inv = jnp.where(idcg > 0.0, 1.0 / jnp.where(idcg > 0.0, idcg, 1.0), 0.0)
    gain_own = jnp.exp2(label_own) - 1.0

    for k in by_distance(nd):
        src = lax.rem(d + k, nd)
        remote(score_s, score_r.at[src], score_ss.at[k], score_rs.at[src], {"docs": src}).wait_recv()
    scores = jnp.concatenate([score_r[i] for i in range(nd)], axis=0)
    sa[0] = scores
    for by in range(1, cap):
        sa[by] = turned(scores, by)

    def soft(by, acc):
        for j in range(nd):
            t = jnp.tanh(sa[by, j : j + 1, :] - scores)
            acc += jnp.where(sm[by, j : j + 1, :] == mark, t, 0.0)
        return acc

    acc = lax.fori_loop(0, cap, soft, jnp.zeros((nd, slots), F32))
    rank = jnp.where(mark > 0.0, 0.5 * (total - 1.0 + acc), 0.0)
    disc = LN2 / jnp.log(2.0 + rank)
    disc_v[...] = disc
    disc_own = disc_v[pl.ds(d, 1), :]
    sd[0] = disc
    for by in range(1, cap):
        sd[by] = turned(disc, by)

    def pairs(by, acc):
        t = jnp.tanh(sa[by] - score_own)
        gap = sg[by] - gain_own
        term = jnp.abs(sd[by] - disc_own) * (gap - jnp.abs(gap) * t)
        return acc + jnp.where(sm[by] == mark_own, term, 0.0)

    acc = lax.fori_loop(0, cap, pairs, jnp.zeros((nd, slots), F32), unroll=2)
    lam_row = 0.5 * inv * jnp.sum(acc, axis=0, keepdims=True)
    lam = jnp.sum(jnp.where(hit_v[...] > 0.0, lam_row, 0.0), axis=1, keepdims=True)

    for h in range(2):
        pg[h] = (lam * slope_v[:, h * half : (h + 1) * half]).astype(BF16)
    pg_send = remote(pg.at[other], pg_in, pair_ss.at[1], pair_rs.at[1], {"sub": other})
    pg_send.start()
    for i in range(width // 128):
        w2_own[i : i + 1, :] = jnp.sum(lam * hid_v[:, i * 128 : (i + 1) * 128], axis=0, keepdims=True)
    w2_x[m] = w2_own[...]
    pg_send.wait_recv()
    both = jnp.concatenate([pg[s], pg_in[...]], axis=0)

    right, left = {"mp": lax.rem(m + 1, nm)}, {"mp": lax.rem(m + nm - 1, nm)}
    far = nm // 2

    def product(rel):
        g_v[rel] = jnp.dot(emb_t[lax.rem(m + rel, nm)], both, preferred_element_type=F32)

    x_sends = []

    def ring_send(side, step, q, value):
        x_s[side, step, q] = value.astype(BF16)
        copy = remote(
            x_s.at[side, step, q], x_r.at[side, step, q], x_ss.at[side, step, q], x_rs.at[side, step, q],
            (right, left)[side],
        )
        copy.start()
        x_sends.append(copy)

    def ring_recv(side, step, q):
        remote(
            x_s.at[side, step, q], x_r.at[side, step, q], x_ss.at[side, step, q], x_rs.at[side, step, q],
            (right, left)[side],
        ).wait_recv()
        return x_r[side, step, q].astype(F32)

    def own(rel, q):
        return g_v[rel, :, q * piece : (q + 1) * piece]

    def rel_of(side, step):
        away = far - step
        return away if side == 0 else (nm - away) % nm

    def long_way(side, q):
        return (q < NQ // 2) == (side == 0)

    product(far)
    for side in range(2):
        for q in range(NQ):
            if long_way(side, q):
                ring_send(side, 0, q, own(far, q))
    for side in range(2):
        product(rel_of(side, 1))
        for q in range(NQ):
            if not long_way(side, q):
                ring_send(side, 1, q, own(rel_of(side, 1), q))
    for step in range(2, far):
        for side in range(2):
            product(rel_of(side, step))
    product(0)

    w2x_sends = []
    for k in by_distance(nm):
        copy = remote(w2_own, w2_x.at[m], w2x_ss.at[k], w2x_rs.at[m], {"mp": lax.rem(m + k, nm)})
        copy.start()
        w2x_sends.append(copy)

    order = list(range(NQ))
    for q in order:
        for side in range(2):
            if long_way(side, q):
                ring_send(side, 1, q, ring_recv(side, 0, q) + own(rel_of(side, 1), q))
    for step in range(2, far):
        for q in order:
            for side in range(2):
                ring_send(side, step, q, ring_recv(side, step - 1, q) + own(rel_of(side, step), q))

    for k in by_distance(nm):
        src = lax.rem(m + k, nm)
        remote(w2_own, w2_x.at[src], w2x_ss.at[k], w2x_rs.at[src], {"mp": src}).wait_recv()
    w2_sum[0] = functools.reduce(lambda a, b: a + b, [w2_x[i] for i in range(nm)])
    w2_pair = remote(w2_sum.at[0], w2_in, pair_ss.at[2], pair_rs.at[2], {"sub": other})
    w2_pair.start()

    z_sends = []
    for q in order:
        block = own(0, q)
        for side in range(2):
            block = block + ring_recv(side, far - 1, q)
        z_s[q] = block.reshape(nd // 2, 16, piece).astype(BF16)
        z, par = q // 2, q % 2

        @pl.when(lax.rem(d, 2) == par)
        def _():
            z_r[z, d] = z_s[q, d // 2]

        for k in by_distance(nd):
            to = lax.rem(d + k, nd)
            copy = remote(z_s.at[q, to // 2], z_r.at[z, d], z_ss.at[z, k], z_rs.at[z, d], {"docs": to})
            z_sends.append((copy, to, par))
            pl.when(lax.rem(to, 2) == par)(copy.start)
        if q == 1:
            w2_pair.wait_recv()
            w2_sum[1] = w2_sum[0] + w2_in[...]
            w2_z[d] = w2_sum[1]
            w2z_sends = []
            for k in by_distance(nd):
                copy = remote(
                    w2_sum.at[1], w2_z.at[d], w2z_ss.at[k], w2z_rs.at[d], {"docs": lax.rem(d + k, nd)}
                )
                copy.start()
                w2z_sends.append(copy)

    grad = lax.dot_general(
        pg[0], w1_v[:, :half], (((1,), (1,)), ((), ())), preferred_element_type=F32
    ) + lax.dot_general(pg[1], w1_v[:, half:], (((1,), (1,)), ((), ())), preferred_element_type=F32)
    eg_v[...] = grad.astype(BF16)
    eg_out = pltpu.make_async_copy(eg_v, eg_h, out_sem.at[0])
    eg_out.start()
    return (
        d, m, s, other, nd, cap, half, z_sends, w2z_sends, x_sends, w2x_sends, score_sends, meta_sends,
        emb_send, pg_send, w2_pair, eg_out,
    )


def whole_kernel(nd, nm, rows, width, cap, *refs):
    state = step_kernel(nd, nm, rows, width, cap, *refs)
    (
        d, m, s, other, nd, cap, half, z_sends, w2z_sends, x_sends, w2x_sends, score_sends, meta_sends,
        emb_send, pg_send, w2_pair, eg_out,
    ) = state
    (
        emb_h, own_h, qry_h, lab_h, w1_h, w2_h,
        eg_h, wg_h, w2g_h,
        emb_v, own_v, qry_v, lab_v, w1_v, w2_v,
        slope_v, hid_v, hit_v,
        meta_s, meta_r, score_s, score_r,
        sa, sm, sg, sd, disc_v,
        embp_v, emb_t, pg, pg_in, g_v,
        x_s, x_r, z_s, z_r, z_f, ag_r, out_v, eg_v,
        w2_own, w2_x, w2_sum, w2_in, w2_z, w2_out,
        load_sem, out_sem, meta_ss, meta_rs, score_ss, score_rs,
        pair_ss, pair_rs, x_ss, x_rs, z_ss, z_rs, ag_ss, ag_rs,
        w2x_ss, w2x_rs, w2z_ss, w2z_rs,
    ) = refs
    part = nd // 2
    core = d // part
    mine = lax.rem(d, part)
    ag_sends = []
    for z in range(2):
        for k in by_distance(nd):
            src = lax.rem(d + k, nd)
            remote(z_s.at[0, 0], z_r.at[z, src], z_ss.at[z, k], z_rs.at[z, src], {"docs": src}).wait_recv()
        z_f[z] = functools.reduce(lambda a, b: a + b, [z_r[z, i].astype(F32) for i in range(nd)]).astype(BF16)

        @pl.when(core == s)
        def _():
            ag_r[s, z, mine] = z_f[z]

        for k in by_distance(nd) + [0]:
            copy = remote(
                z_f.at[z], ag_r.at[s, z, mine], ag_ss.at[z, k], ag_rs.at[s, z, mine],
                {"docs": lax.rem(d + k, nd), "sub": core},
            )
            if k == 0:
                pl.when(core != s)(copy.start)
            else:
                copy.start()
            ag_sends.append((copy, k))

    for k in by_distance(nd):
        src = lax.rem(d + k, nd)
        remote(w2_sum.at[1], w2_z.at[src], w2z_ss.at[k], w2z_rs.at[src], {"docs": src}).wait_recv()
    w2_out[...] = functools.reduce(lambda a, b: a + b, [w2_z[i] for i in range(nd)])
    w2_copy = pltpu.make_async_copy(w2_out, w2g_h, out_sem.at[1])
    w2_copy.start()

    for z in range(2):
        for src in range(2):
            for k in range(part):
                copy = remote(
                    z_f.at[z], ag_r.at[src, z, k], ag_ss.at[z, k], ag_rs.at[src, z, k], {"sub": other}
                )
                same = (src == s) & (s * part + k == d)
                pl.when(jnp.logical_not(same))(copy.wait_recv)
                out_v[(k // 2) * 16 : (k // 2) * 16 + 16, pl.ds(src * half + z * 256 + (k % 2) * 128, 128)] = ag_r[
                    src, z, k
                ].astype(F32)
    wg_copy = pltpu.make_async_copy(out_v, wg_h, out_sem.at[2])
    wg_copy.start()

    for copy in score_sends + meta_sends + [emb_send, pg_send, w2_pair] + x_sends + w2x_sends + w2z_sends:
        copy.wait_send()
    for copy, to, par in z_sends:
        pl.when(lax.rem(to, 2) == par)(copy.wait_send)
    for copy, k in ag_sends:
        if k == 0:
            pl.when(core != s)(copy.wait_send)
        else:
            copy.wait_send()
    eg_out.wait()
    w2_copy.wait()
    wg_copy.wait()


def solution(mesh):
    nd, nm = mesh.shape["docs"], mesh.shape["mp"]

    def on_device(embeddings, owner_shard, query_local, labels, w_first, w_second):
        rows, width = embeddings.shape
        cap = 2 * rows // nd
        slots = nd * cap
        half = width // 2
        piece = half // NQ
        far = nm // 2
        dma = pltpu.SemaphoreType.DMA
        any_spec = pl.BlockSpec(memory_space=pl.ANY)
        scratch = [
            pltpu.VMEM((rows, width), BF16),
            pltpu.VMEM((1, rows), jnp.int32),
            pltpu.VMEM((1, rows), jnp.int32),
            pltpu.VMEM((1, rows), jnp.int32),
            pltpu.VMEM((width, width), BF16),
            pltpu.VMEM((1, width), F32),
            pltpu.VMEM((rows, width), F32),
            pltpu.VMEM((rows, width), F32),
            pltpu.VMEM((rows, slots), F32),
            pltpu.VMEM((2, slots), BF16),
            pltpu.VMEM((nd, 2, slots), BF16),
            pltpu.VMEM((1, slots), F32),
            pltpu.VMEM((nd, 1, slots), F32),
            pltpu.VMEM((cap, nd, slots), F32),
            pltpu.VMEM((cap, nd, slots), F32),
            pltpu.VMEM((cap, nd, slots), F32),
            pltpu.VMEM((cap, nd, slots), F32),
            pltpu.VMEM((nd, slots), F32),
            pltpu.VMEM((rows, width), BF16),
            pltpu.VMEM((nm, width // nm, 2 * rows), BF16),
            pltpu.VMEM((2, rows, half), BF16),
            pltpu.VMEM((rows, half), BF16),
            pltpu.VMEM((nm, width // nm, half), F32),
            pltpu.VMEM((2, far, NQ, width // nm, piece), BF16),
            pltpu.VMEM((2, far, NQ, width // nm, piece), BF16),
            pltpu.VMEM((NQ, nd // 2, 16, piece), BF16),
            pltpu.VMEM((2, nd, 16, piece), BF16),
            pltpu.VMEM((2, 16, piece), BF16),
            pltpu.VMEM((2, 2, nd // 2, 16, piece), BF16),
            pltpu.VMEM((width // nm // 2, width), F32),
            pltpu.VMEM((rows, width), BF16),
            pltpu.VMEM((width // 128, 128), F32),
            pltpu.VMEM((nm, width // 128, 128), F32),
            pltpu.VMEM((2, width // 128, 128), F32),
            pltpu.VMEM((width // 128, 128), F32),
            pltpu.VMEM((nd, width // 128, 128), F32),
            pltpu.VMEM((width // 128, 128), F32),
            dma((5 + FWD,)),
            dma((3,)),
            dma((nd,)),
            dma((nd,)),
            dma((nd,)),
            dma((nd,)),
            dma((3,)),
            dma((3,)),
            dma((2, far, NQ)),
            dma((2, far, NQ)),
            dma((2, nd)),
            dma((2, nd)),
            dma((2, nd)),
            dma((2, 2, nd // 2)),
            dma((nm,)),
            dma((nm,)),
            dma((nd,)),
            dma((nd,)),
        ]
        emb_grad, w_first_grad, w_second_grad = pl.pallas_call(
            functools.partial(whole_kernel, nd, nm, rows, width, cap),
            out_shape=(
                jax.ShapeDtypeStruct((rows, width), BF16),
                jax.ShapeDtypeStruct((width // nm // 2, width), F32),
                jax.ShapeDtypeStruct((width // 128, 128), F32),
            ),
            in_specs=[any_spec] * 6,
            out_specs=(any_spec,) * 3,
            scratch_shapes=scratch,
            compiler_params=pltpu.CompilerParams(
                collective_id=0, has_side_effects=True, vmem_limit_bytes=48 * 1024 * 1024
            ),
            name="ranking_step",
        )(
            embeddings,
            owner_shard.reshape(1, rows),
            query_local.reshape(1, rows),
            labels.reshape(1, rows),
            w_first,
            w_second.reshape(1, width),
        )
        return emb_grad, w_first_grad, w_second_grad.reshape(width)

    whole = ("groups", "docs", "mp", "sub")
    return jax.shard_map(
        on_device,
        mesh=mesh,
        in_specs=(P(whole, None), P(whole, None), P(whole), P(whole), P(), P()),
        out_specs=(P(whole, None), P(("groups", "mp", "sub"), None), P("groups")),
        check_vma=False,
    )
```

time: 306 us -> 105 us (0.34)
  blocking collectives: 195 us -> 0 us
  Pallas kernels: 0 us -> 96.6 us
  starting transfers between devices: 56.9 us -> 0 us
  waiting for transfers between devices: 28.6 us -> 0 us
  other arithmetic: 10 us -> 0 us
  matrix products: 5.27 us -> 0 us
    psum x3 -> x0, blocking collectives: 133 us -> none  [one_axis_at_a_time(): return functools.reduce(lax.psum, axes, x)]
    pallas_call x0 -> x1, Pallas kernels: none -> 96.6 us  [on_device(): pl.pallas_call(functools.partial(whole_kernel, nd, nm, rows, width, cap),...]
    all_to_all x1 -> x0, blocking collectives: 62.4 us -> none  [summed_on_arrival(): lax.all_to_all(tiles, axis, split_axis=0, concat_axis=0, tiled=True)]
    all_to_all x4 -> x0, starting transfers between devices: 56.9 us -> none  [the longest x1 44.2 us: on_device(): lax.all_to_all(outgoing, 'docs', split_axis=0, concat_axis=0, tiled=True)]
    all_to_all x4 -> x0, waiting for transfers between devices: 28.6 us -> none  [the longest x1 10.8 us: on_device(): lax.all_to_all(slot_lambdas.reshape(doc_count, capacity), 'docs', split_a...]
    unnamed x8 -> x15, local copies, waits for them, and re-layouts: 0.02 us -> 7.18 us
    reduce_sum x5 -> x0, other arithmetic: 6.3 us -> none  [the longest x1 2.71 us: of_everyone(): return sent_to_all(x, axis).astype(jnp.float32).sum(axis=0)]
    dot_general x7 -> x0, matrix products: 5.27 us -> none  [the longest x1 1.54 us: on_device(): lax.dot_general(pre_grad, w_first, (((1,), (1,)), ((), ())), preferred_el...]
  transfers between devices with their start and end apart: 4 -> 0, of which waited for: 3 -> 0; matrix products, arithmetic and copies ran while one was open for 2% -> 0% of each run, Pallas kernels for 0% -> 0%
where the time goes in v1:
time: 105 us; the launch traced here: 104 us
  Pallas kernels  96.6 us (92%)
  local copies, waits for them, and re-layouts  7.18 us (7%)
    pallas_call x1, Pallas kernels, on_device(): pl.pallas_call(functools.partial(whole_kernel, nd, nm, rows, width, cap),...  96.6 us
    unnamed x15, local copies, waits for them, and re-layouts  7.18 us

profile of v1, /device:TPU:65, one launch (start us, length us, event | category | flops | bytes accessed | tf_op | source)
XLA Modules:
  0.0 104.5 jit_solution(9925060114231429058)
XLA Ops:
  0.6 0.0 copy-start
  0.6 1.6 %copy-done = bf16[1024,1024]{1,0:T(8,128)(2,1)S(1)} copy-done((bf16[1024,1024]{1,0:T(8,128)(2,1)S(1)}, bf16[1024,1024]{1,0:T(8,128)(2,1)}, u32[]{:S(2)}) %copy-start) | copy-done | bytes 2097176
  2.2 0.0 copy-start.1
  2.2 0.9 copy-done.1
  3.2 0.0 copy-start.2
  3.2 0.7 copy-done.2
  3.9 0.0 copy-start.3
  3.9 0.7 copy-done.3
  4.5 0.0 copy-start.4
  4.5 0.7 copy-done.4
  5.2 0.0 copy-start.5
  5.2 0.7 copy-done.5
  5.8 96.6 %ranking_step.1 = (bf16[128,1024]{1,0:T(8,128)(2,1)S(1)}, f32[64,1024]{1,0:T(8,128)S(1)}, f32[8,128]{1,0:T(8,128)S(1)}) custom-call(bf16[128,1024]{1,0:T(8,128)(2,1)S(1)} %copy-done.1, s32[1,128]{1,0:T(1,128)S(1)} %bitcast.7, s32[1,128]{1,0:T(1,128)S(1)} %bitcast.8, s32[1,128]{1,0:T(1,128)S(1)} %bitcast.9, bf16[1024,1024]{1,0:T(8,128)(2,1)S(1)} %copy-done, ...), custom_call_target="tpu_custom_call" | custom-call | tf_op jit(solution)/shard_map/ranking_step/pallas_call | solution.py:495
  102.5 0.7 copy.12
  103.2 0.7 copy.13
  103.9 0.6 copy.14
Async XLA Ops:
  0.6 1.6 %copy-start = (bf16[1024,1024]{1,0:T(8,128)(2,1)S(1)}, bf16[1024,1024]{1,0:T(8,128)(2,1)}, u32[]{:S(2)}) copy-start(bf16[1024,1024]{1,0:T(8,128)(2,1)} %refs_4_.1) | copy-start | bytes 6291460
  2.2 0.9 copy-start.1
  3.2 0.7 copy-start.2
  3.9 0.7 copy-start.3
  4.5 0.7 copy-start.4
  5.2 0.7 copy-start.5

commit v2 on v1

--- a/solution.py
+++ b/solution.py
@@ -23,6 +23,18 @@
     )
 
 
+class Phases:
+    def __init__(self):
+        self.scope = None
+
+    def __call__(self, name):
+        if self.scope is not None:
+            self.scope.__exit__(None, None, None)
+        self.scope = jax.named_scope(name) if name else None
+        if self.scope is not None:
+            self.scope.__enter__()
+
+
 def by_distance(count):
     return sorted(range(1, count), key=lambda k: -min(k, count - k))
 
@@ -30,15 +42,15 @@
 def step_kernel(
     nd, nm, rows, width, cap,
     emb_h, own_h, qry_h, lab_h, w1_h, w2_h,
-    eg_h, wg_h, w2g_h,
+    eg_v, out_v, w2_out,
     emb_v, own_v, qry_v, lab_v, w1_v, w2_v,
     slope_v, hid_v, hit_v,
     meta_s, meta_r, score_s, score_r,
     sa, sm, sg, sd, disc_v,
     embp_v, emb_t, pg, pg_in, g_v,
-    x_s, x_r, z_s, z_r, z_f, ag_r, out_v, eg_v,
-    w2_own, w2_x, w2_sum, w2_in, w2_z, w2_out,
-    load_sem, out_sem, meta_ss, meta_rs, score_ss, score_rs,
+    x_s, x_r, z_s, z_r, z_f, ag_r,
+    w2_own, w2_x, w2_sum, w2_in, w2_z,
+    load_sem, meta_ss, meta_rs, score_ss, score_rs,
     pair_ss, pair_rs, x_ss, x_rs, z_ss, z_rs, ag_ss, ag_rs,
     w2x_ss, w2x_rs, w2z_ss, w2z_rs,
 ):
@@ -50,6 +62,8 @@
     half = width // 2
     piece = half // NQ
 
+    phase = Phases()
+    phase("greet")
     barrier = pltpu.get_barrier_semaphore()
     for k in by_distance(nd):
         for core in (s, other):
@@ -74,6 +88,7 @@
     for copy in loads + w_loads:
         copy.start()
 
+    phase("own_slots")
     for copy in loads[:3]:
         copy.wait()
     row_i = lax.broadcasted_iota(jnp.int32, (rows, rows), 0)
@@ -102,6 +117,7 @@
     meta_r[d, 0:1, :] = mark_own.astype(BF16)
     meta_r[d, 1:2, :] = label_own.astype(BF16)
 
+    phase("scorer")
     for copy in loads[3:]:
         copy.wait()
     score = jnp.zeros((rows, 1), F32)
@@ -119,8 +135,10 @@
     score_s[...] = score_own
     score_r[d] = score_own
 
+    phase("barrier")
     pl.semaphore_wait(barrier, 2 * (nd - 1) + (nm - 1) + 1)
 
+    phase("send_scores")
     score_sends, meta_sends = [], []
     for k in by_distance(nd):
         where = {"docs": lax.rem(d + k, nd)}
@@ -131,6 +149,7 @@
     emb_send = remote(emb_v, embp_v, pair_ss.at[0], pair_rs.at[0], {"sub": other})
     emb_send.start()
 
+    phase("turn")
     def turn(block, at):
         for c in range(nm):
             w = width // nm
@@ -142,9 +161,11 @@
     emb_send.wait_recv()
     turn(embp_v, 1)
 
+    phase("meta_wait")
     for k in by_distance(nd):
         src = lax.rem(d + k, nd)
         remote(meta_s, meta_r.at[src], meta_ss.at[k], meta_rs.at[src], {"docs": src}).wait_recv()
+    phase("meta_work")
     lane = lax.broadcasted_iota(jnp.int32, (nd, slots), 1)
     in_group = lax.rem(lane, cap)
 
@@ -187,9 +208,11 @@
     inv = jnp.where(idcg > 0.0, 1.0 / jnp.where(idcg > 0.0, idcg, 1.0), 0.0)
     gain_own = jnp.exp2(label_own) - 1.0
 
+    phase("score_wait")
     for k in by_distance(nd):
         src = lax.rem(d + k, nd)
         remote(score_s, score_r.at[src], score_ss.at[k], score_rs.at[src], {"docs": src}).wait_recv()
+    phase("soft_rank")
     scores = jnp.concatenate([score_r[i] for i in range(nd)], axis=0)
     sa[0] = scores
     for by in range(1, cap):
@@ -210,6 +233,7 @@
     for by in range(1, cap):
         sd[by] = turned(disc, by)
 
+    phase("lambdas")
     def pairs(by, acc):
         t = jnp.tanh(sa[by] - score_own)
         gap = sg[by] - gain_own
@@ -220,6 +244,7 @@
     lam_row = 0.5 * inv * jnp.sum(acc, axis=0, keepdims=True)
     lam = jnp.sum(jnp.where(hit_v[...] > 0.0, lam_row, 0.0), axis=1, keepdims=True)
 
+    phase("pre_grad")
     for h in range(2):
         pg[h] = (lam * slope_v[:, h * half : (h + 1) * half]).astype(BF16)
     pg_send = remote(pg.at[other], pg_in, pair_ss.at[1], pair_rs.at[1], {"sub": other})
@@ -227,6 +252,7 @@
     for i in range(width // 128):
         w2_own[i : i + 1, :] = jnp.sum(lam * hid_v[:, i * 128 : (i + 1) * 128], axis=0, keepdims=True)
     w2_x[m] = w2_own[...]
+    phase("pair_wait")
     pg_send.wait_recv()
     both = jnp.concatenate([pg[s], pg_in[...]], axis=0)
 
@@ -264,6 +290,7 @@
     def long_way(side, q):
         return (q < NQ // 2) == (side == 0)
 
+    phase("products")
     product(far)
     for side in range(2):
         for q in range(NQ):
@@ -279,6 +306,7 @@
             product(rel_of(side, step))
     product(0)
 
+    phase("ring")
     w2x_sends = []
     for k in by_distance(nm):
         copy = remote(w2_own, w2_x.at[m], w2x_ss.at[k], w2x_rs.at[m], {"mp": lax.rem(m + k, nm)})
@@ -295,6 +323,7 @@
             for side in range(2):
                 ring_send(side, step, q, ring_recv(side, step - 1, q) + own(rel_of(side, step), q))
 
+    phase("w2_x")
     for k in by_distance(nm):
         src = lax.rem(m + k, nm)
         remote(w2_own, w2_x.at[src], w2x_ss.at[k], w2x_rs.at[src], {"mp": src}).wait_recv()
@@ -302,6 +331,7 @@
     w2_pair = remote(w2_sum.at[0], w2_in, pair_ss.at[2], pair_rs.at[2], {"sub": other})
     w2_pair.start()
 
+    phase("ring_end")
     z_sends = []
     for q in order:
         block = own(0, q)
@@ -331,38 +361,12 @@
                 copy.start()
                 w2z_sends.append(copy)
 
+    phase("emb_grad")
     grad = lax.dot_general(
         pg[0], w1_v[:, :half], (((1,), (1,)), ((), ())), preferred_element_type=F32
     ) + lax.dot_general(pg[1], w1_v[:, half:], (((1,), (1,)), ((), ())), preferred_element_type=F32)
     eg_v[...] = grad.astype(BF16)
-    eg_out = pltpu.make_async_copy(eg_v, eg_h, out_sem.at[0])
-    eg_out.start()
-    return (
-        d, m, s, other, nd, cap, half, z_sends, w2z_sends, x_sends, w2x_sends, score_sends, meta_sends,
-        emb_send, pg_send, w2_pair, eg_out,
-    )
-
-
-def whole_kernel(nd, nm, rows, width, cap, *refs):
-    state = step_kernel(nd, nm, rows, width, cap, *refs)
-    (
-        d, m, s, other, nd, cap, half, z_sends, w2z_sends, x_sends, w2x_sends, score_sends, meta_sends,
-        emb_send, pg_send, w2_pair, eg_out,
-    ) = state
-    (
-        emb_h, own_h, qry_h, lab_h, w1_h, w2_h,
-        eg_h, wg_h, w2g_h,
-        emb_v, own_v, qry_v, lab_v, w1_v, w2_v,
-        slope_v, hid_v, hit_v,
-        meta_s, meta_r, score_s, score_r,
-        sa, sm, sg, sd, disc_v,
-        embp_v, emb_t, pg, pg_in, g_v,
-        x_s, x_r, z_s, z_r, z_f, ag_r, out_v, eg_v,
-        w2_own, w2_x, w2_sum, w2_in, w2_z, w2_out,
-        load_sem, out_sem, meta_ss, meta_rs, score_ss, score_rs,
-        pair_ss, pair_rs, x_ss, x_rs, z_ss, z_rs, ag_ss, ag_rs,
-        w2x_ss, w2x_rs, w2z_ss, w2z_rs,
-    ) = refs
+    phase("docs_sum")
     part = nd // 2
     core = d // part
     mine = lax.rem(d, part)
@@ -388,13 +392,13 @@
                 copy.start()
             ag_sends.append((copy, k))
 
+    phase("w2_z")
     for k in by_distance(nd):
         src = lax.rem(d + k, nd)
         remote(w2_sum.at[1], w2_z.at[src], w2z_ss.at[k], w2z_rs.at[src], {"docs": src}).wait_recv()
     w2_out[...] = functools.reduce(lambda a, b: a + b, [w2_z[i] for i in range(nd)])
-    w2_copy = pltpu.make_async_copy(w2_out, w2g_h, out_sem.at[1])
-    w2_copy.start()
-
+
+    phase("docs_gather")
     for z in range(2):
         for src in range(2):
             for k in range(part):
@@ -406,9 +410,8 @@
                 out_v[(k // 2) * 16 : (k // 2) * 16 + 16, pl.ds(src * half + z * 256 + (k % 2) * 128, 128)] = ag_r[
                     src, z, k
                 ].astype(F32)
-    wg_copy = pltpu.make_async_copy(out_v, wg_h, out_sem.at[2])
-    wg_copy.start()
-
+
+    phase("drain")
     for copy in score_sends + meta_sends + [emb_send, pg_send, w2_pair] + x_sends + w2x_sends + w2z_sends:
         copy.wait_send()
     for copy, to, par in z_sends:
@@ -418,9 +421,15 @@
             pl.when(core != s)(copy.wait_send)
         else:
             copy.wait_send()
-    eg_out.wait()
-    w2_copy.wait()
-    wg_copy.wait()
+    phase(None)
+
+
+def write_out(a, b, c, a_out, b_out, c_out, sem):
+    copies = [pltpu.make_async_copy(x, y, sem.at[i]) for i, (x, y) in enumerate(((a, a_out), (b, b_out), (c, c_out)))]
+    for copy in copies:
+        copy.start()
+    for copy in copies:
+        copy.wait()
 
 
 def solution(mesh):
@@ -434,7 +443,7 @@
         piece = half // NQ
         far = nm // 2
         dma = pltpu.SemaphoreType.DMA
-        any_spec = pl.BlockSpec(memory_space=pl.ANY)
+        hbm, vmem, anywhere = (pl.BlockSpec(memory_space=a) for a in (pltpu.HBM, pltpu.VMEM, pl.ANY))
         scratch = [
             pltpu.VMEM((rows, width), BF16),
             pltpu.VMEM((1, rows), jnp.int32),
@@ -465,16 +474,12 @@
             pltpu.VMEM((2, nd, 16, piece), BF16),
             pltpu.VMEM((2, 16, piece), BF16),
             pltpu.VMEM((2, 2, nd // 2, 16, piece), BF16),
-            pltpu.VMEM((width // nm // 2, width), F32),
-            pltpu.VMEM((rows, width), BF16),
             pltpu.VMEM((width // 128, 128), F32),
             pltpu.VMEM((nm, width // 128, 128), F32),
             pltpu.VMEM((2, width // 128, 128), F32),
             pltpu.VMEM((width // 128, 128), F32),
             pltpu.VMEM((nd, width // 128, 128), F32),
-            pltpu.VMEM((width // 128, 128), F32),
             dma((5 + FWD,)),
-            dma((3,)),
             dma((nd,)),
             dma((nd,)),
             dma((nd,)),
@@ -492,28 +497,43 @@
             dma((nd,)),
             dma((nd,)),
         ]
-        emb_grad, w_first_grad, w_second_grad = pl.pallas_call(
-            functools.partial(whole_kernel, nd, nm, rows, width, cap),
-            out_shape=(
-                jax.ShapeDtypeStruct((rows, width), BF16),
-                jax.ShapeDtypeStruct((width // nm // 2, width), F32),
-                jax.ShapeDtypeStruct((width // 128, 128), F32),
-            ),
-            in_specs=[any_spec] * 6,
-            out_specs=(any_spec,) * 3,
+        shapes = (
+            jax.ShapeDtypeStruct((rows, width), BF16),
+            jax.ShapeDtypeStruct((width // nm // 2, width), F32),
+            jax.ShapeDtypeStruct((width // 128, 128), F32),
+        )
+        results = pl.pallas_call(
+            functools.partial(step_kernel, nd, nm, rows, width, cap),
+            out_shape=tuple(pltpu.VMEM(a.shape, a.dtype) for a in shapes),
+            in_specs=[hbm] * 6,
+            out_specs=(vmem,) * 3,
             scratch_shapes=scratch,
             compiler_params=pltpu.CompilerParams(
-                collective_id=0, has_side_effects=True, vmem_limit_bytes=48 * 1024 * 1024
+                collective_id=0, has_side_effects=True, vmem_limit_bytes=40 * 1024 * 1024
             ),
             name="ranking_step",
         )(
-            embeddings,
-            owner_shard.reshape(1, rows),
-            query_local.reshape(1, rows),
-            labels.reshape(1, rows),
-            w_first,
-            w_second.reshape(1, width),
+            *(
+                pltpu.with_memory_space_constraint(a, pltpu.HBM)
+                for a in (
+                    embeddings,
+                    owner_shard.reshape(1, rows),
+                    query_local.reshape(1, rows),
+                    labels.reshape(1, rows),
+                    w_first,
+                    w_second.reshape(1, width),
+                )
+            )
         )
+        emb_grad, w_first_grad, w_second_grad = pl.pallas_call(
+            write_out,
+            out_shape=shapes,
+            in_specs=[anywhere] * 3,
+            out_specs=(hbm,) * 3,
+            scratch_shapes=[dma((3,))],
+            compiler_params=pltpu.CompilerParams(vmem_limit_bytes=1024 * 1024),
+            name="write_out",
+        )(*results)
         return emb_grad, w_first_grad, w_second_grad.reshape(width)
 
     whole = ("groups", "docs", "mp", "sub")

time: 105 us -> 98.1 us (0.934)
  local copies, waits for them, and re-layouts: 7.18 us -> 0 us
    unnamed x15 -> x0, local copies, waits for them, and re-layouts: 7.18 us -> none
    pallas_call x1 -> x2, Pallas kernels: 96.6 us -> 97.4 us  [the longest x1 96.5 us: on_device(): pl.pallas_call(functools.partial(step_kernel, nd, nm, rows, width, cap),...]
where the time goes in v2:
time: 98.1 us; the launch traced here: 98 us
  Pallas kernels  97.4 us (99%)
    pallas_call x1, Pallas kernels, on_device(): pl.pallas_call(functools.partial(step_kernel, nd, nm, rows, width, cap),...  96.5 us

profile of v2, /device:TPU:65, one launch (start us, length us, event | category | flops | bytes accessed | tf_op | source)
XLA Modules:
  0.0 98.0 jit_solution(9618293797112433914)
XLA Ops:
  0.6 96.5 %ranking_step.1 = (bf16[128,1024]{1,0:T(8,128)(2,1)S(1)}, f32[64,1024]{1,0:T(8,128)S(1)}, f32[8,128]{1,0:T(8,128)S(1)}) custom-call(bf16[128,1024]{1,0:T(8,128)(2,1)} %emb_h.1, s32[1,128]{1,0:T(1,128)} %bitcast.6, s32[1,128]{1,0:T(1,128)} %bitcast.7, s32[1,128]{1,0:T(1,128)} %bitcast.8, bf16[1024,1024]{1,0:T(8,128)(2,1)} %w1_h.1, f32[1,1024]{1,0:T(1,128)} %bitcast.5), custom_call_target="tpu_custom_call" | custom-call | tf_op jit(solution)/shard_map/ranking_step/pallas_call | solution.py:505
  97.2 0.8 write_out.1

commit v3 on v2

--- a/solution.py
+++ b/solution.py
@@ -46,7 +46,7 @@
     emb_v, own_v, qry_v, lab_v, w1_v, w2_v,
     slope_v, hid_v, hit_v,
     meta_s, meta_r, score_s, score_r,
-    sa, sm, sg, sd, disc_v,
+    sa, sm, sg, sd,
     embp_v, emb_t, pg, pg_in, g_v,
     x_s, x_r, z_s, z_r, z_f, ag_r,
     w2_own, w2_x, w2_sum, w2_in, w2_z,
@@ -64,14 +64,6 @@
 
     phase = Phases()
     phase("greet")
-    barrier = pltpu.get_barrier_semaphore()
-    for k in by_distance(nd):
-        for core in (s, other):
-            pl.semaphore_signal(barrier, inc=1, device_id={"docs": lax.rem(d + k, nd), "sub": core}, device_id_type=MESH)
-    for k in by_distance(nm):
-        pl.semaphore_signal(barrier, inc=1, device_id={"mp": lax.rem(m + k, nm)}, device_id_type=MESH)
-    pl.semaphore_signal(barrier, inc=1, device_id={"sub": other}, device_id_type=MESH)
-
     loads = [
         pltpu.make_async_copy(a, b, load_sem.at[i])
         for i, (a, b) in enumerate(
@@ -88,6 +80,15 @@
     for copy in loads + w_loads:
         copy.start()
 
+    reach = nd // 4
+    barrier = pltpu.get_barrier_semaphore()
+    near = [k for k in by_distance(nd) if min(k, nd - k) <= reach]
+    for k in near:
+        pl.semaphore_signal(barrier, inc=1, device_id={"docs": lax.rem(d + k, nd)}, device_id_type=MESH)
+    for k in (1, nm - 1):
+        pl.semaphore_signal(barrier, inc=1, device_id={"mp": lax.rem(m + k, nm)}, device_id_type=MESH)
+    pl.semaphore_signal(barrier, inc=1, device_id={"sub": other}, device_id_type=MESH)
+
     phase("own_slots")
     for copy in loads[:3]:
         copy.wait()
@@ -114,12 +115,42 @@
     label_own = slotted(upright(lab_v[...].astype(F32)))
     meta_s[0:1, :] = mark_own.astype(BF16)
     meta_s[1:2, :] = label_own.astype(BF16)
-    meta_r[d, 0:1, :] = mark_own.astype(BF16)
-    meta_r[d, 1:2, :] = label_own.astype(BF16)
-
+    meta_r[0, 0:1, :] = mark_own.astype(BF16)
+    meta_r[0, 1:2, :] = label_own.astype(BF16)
+
+    def to_near(src, dst, send_sem, recv_sem):
+        copies = []
+        for k in near:
+            copies.append(remote(src, dst.at[nd - k], send_sem.at[k], recv_sem.at[nd - k], {"docs": lax.rem(d + k, nd)}))
+            copies[-1].start()
+        return copies
+
+    def from_near(src, dst, send_sem, recv_sem):
+        for k in near:
+            remote(src, dst.at[k], send_sem.at[k], recv_sem.at[k], {"docs": lax.rem(d + k, nd)}).wait_recv()
+
+    def relays(dst, send_sem, recv_sem):
+        ahead, behind = {"docs": lax.rem(d + reach, nd)}, {"docs": lax.rem(d + nd - reach, nd)}
+        return [
+            remote(
+                dst.at[pl.ds(nd - reach, reach)], dst.at[pl.ds(nd - 2 * reach, reach)],
+                send_sem.at[nd - 2 * reach], recv_sem.at[nd - 2 * reach], ahead,
+            ),
+            remote(
+                dst.at[pl.ds(1, reach - 1)], dst.at[pl.ds(reach + 1, reach - 1)],
+                send_sem.at[reach + 1], recv_sem.at[reach + 1], behind,
+            ),
+        ]
+
+
+    phase("barrier")
+    pl.semaphore_wait(barrier, len(near) + 3)
+    meta_sends = to_near(meta_s, meta_r, meta_ss, meta_rs)
     phase("scorer")
     for copy in loads[3:]:
         copy.wait()
+    emb_send = remote(emb_v, embp_v, pair_ss.at[0], pair_rs.at[0], {"sub": other})
+    emb_send.start()
     score = jnp.zeros((rows, 1), F32)
     for i in range(FWD):
         w_loads[i].wait()
@@ -133,22 +164,13 @@
         slope_v[:, at] = w2 * (sig * (1.0 + pre * (1.0 - sig)))
     score_own = slotted(0.5 * score)
     score_s[...] = score_own
-    score_r[d] = score_own
-
-    phase("barrier")
-    pl.semaphore_wait(barrier, 2 * (nd - 1) + (nm - 1) + 1)
-
+    score_r[0] = score_own
     phase("send_scores")
-    score_sends, meta_sends = [], []
-    for k in by_distance(nd):
-        where = {"docs": lax.rem(d + k, nd)}
-        meta_sends.append(remote(meta_s, meta_r.at[d], meta_ss.at[k], meta_rs.at[d], where))
-        meta_sends[-1].start()
-        score_sends.append(remote(score_s, score_r.at[d], score_ss.at[k], score_rs.at[d], where))
-        score_sends[-1].start()
-    emb_send = remote(emb_v, embp_v, pair_ss.at[0], pair_rs.at[0], {"sub": other})
-    emb_send.start()
-
+    score_sends = to_near(score_s, score_r, score_ss, score_rs)
+    from_near(meta_s, meta_r, meta_ss, meta_rs)
+    meta_relays = relays(meta_r, meta_ss, meta_rs)
+    for copy in meta_relays:
+        copy.start()
     phase("turn")
     def turn(block, at):
         for c in range(nm):
@@ -161,10 +183,15 @@
     emb_send.wait_recv()
     turn(embp_v, 1)
 
+    phase("near_wait")
+    from_near(score_s, score_r, score_ss, score_rs)
+    score_relays = relays(score_r, score_ss, score_rs)
+    for copy in score_relays:
+        copy.start()
+
     phase("meta_wait")
-    for k in by_distance(nd):
-        src = lax.rem(d + k, nd)
-        remote(meta_s, meta_r.at[src], meta_ss.at[k], meta_rs.at[src], {"docs": src}).wait_recv()
+    for copy in meta_relays:
+        copy.wait_recv()
     phase("meta_work")
     lane = lax.broadcasted_iota(jnp.int32, (nd, slots), 1)
     in_group = lax.rem(lane, cap)
@@ -209,9 +236,8 @@
     gain_own = jnp.exp2(label_own) - 1.0
 
     phase("score_wait")
-    for k in by_distance(nd):
-        src = lax.rem(d + k, nd)
-        remote(score_s, score_r.at[src], score_ss.at[k], score_rs.at[src], {"docs": src}).wait_recv()
+    for copy in score_relays:
+        copy.wait_recv()
     phase("soft_rank")
     scores = jnp.concatenate([score_r[i] for i in range(nd)], axis=0)
     sa[0] = scores
@@ -227,8 +253,7 @@
     acc = lax.fori_loop(0, cap, soft, jnp.zeros((nd, slots), F32))
     rank = jnp.where(mark > 0.0, 0.5 * (total - 1.0 + acc), 0.0)
     disc = LN2 / jnp.log(2.0 + rank)
-    disc_v[...] = disc
-    disc_own = disc_v[pl.ds(d, 1), :]
+    disc_own = disc[0:1, :]
     sd[0] = disc
     for by in range(1, cap):
         sd[by] = turned(disc, by)
@@ -307,12 +332,6 @@
     product(0)
 
     phase("ring")
-    w2x_sends = []
-    for k in by_distance(nm):
-        copy = remote(w2_own, w2_x.at[m], w2x_ss.at[k], w2x_rs.at[m], {"mp": lax.rem(m + k, nm)})
-        copy.start()
-        w2x_sends.append(copy)
-
     order = list(range(NQ))
     for q in order:
         for side in range(2):
@@ -323,14 +342,6 @@
             for side in range(2):
                 ring_send(side, step, q, ring_recv(side, step - 1, q) + own(rel_of(side, step), q))
 
-    phase("w2_x")
-    for k in by_distance(nm):
-        src = lax.rem(m + k, nm)
-        remote(w2_own, w2_x.at[src], w2x_ss.at[k], w2x_rs.at[src], {"mp": src}).wait_recv()
-    w2_sum[0] = functools.reduce(lambda a, b: a + b, [w2_x[i] for i in range(nm)])
-    w2_pair = remote(w2_sum.at[0], w2_in, pair_ss.at[2], pair_rs.at[2], {"sub": other})
-    w2_pair.start()
-
     phase("ring_end")
     z_sends = []
     for q in order:
@@ -349,7 +360,51 @@
             copy = remote(z_s.at[q, to // 2], z_r.at[z, d], z_ss.at[z, k], z_rs.at[z, d], {"docs": to})
             z_sends.append((copy, to, par))
             pl.when(lax.rem(to, 2) == par)(copy.start)
-        if q == 1:
+
+    w2x_sends = []
+    for k in by_distance(nm):
+        copy = remote(w2_own, w2_x.at[m], w2x_ss.at[k], w2x_rs.at[m], {"mp": lax.rem(m + k, nm)})
+        copy.start()
+        w2x_sends.append(copy)
+
+    phase("emb_grad")
+    grad = lax.dot_general(
+        pg[0], w1_v[:, :half], (((1,), (1,)), ((), ())), preferred_element_type=F32
+    ) + lax.dot_general(pg[1], w1_v[:, half:], (((1,), (1,)), ((), ())), preferred_element_type=F32)
+    eg_v[...] = grad.astype(BF16)
+    phase("docs_sum")
+    for k in by_distance(nm):
+        src = lax.rem(m + k, nm)
+        remote(w2_own, w2_x.at[src], w2x_ss.at[k], w2x_rs.at[src], {"mp": src}).wait_recv()
+    w2_sum[0] = functools.reduce(lambda a, b: a + b, [w2_x[i] for i in range(nm)])
+    w2_pair = remote(w2_sum.at[0], w2_in, pair_ss.at[2], pair_rs.at[2], {"sub": other})
+    w2_pair.start()
+
+    part = nd // 2
+    core = d // part
+    mine = lax.rem(d, part)
+    ag_sends = []
+    for z in range(2):
+        for k in by_distance(nd):
+            src = lax.rem(d + k, nd)
+            remote(z_s.at[0, 0], z_r.at[z, src], z_ss.at[z, k], z_rs.at[z, src], {"docs": src}).wait_recv()
+        z_f[z] = functools.reduce(lambda a, b: a + b, [z_r[z, i].astype(F32) for i in range(nd)]).astype(BF16)
+
+        @pl.when(core == s)
+        def _():
+            ag_r[s, z, mine] = z_f[z]
+
+        for k in by_distance(nd) + [0]:
+            copy = remote(
+                z_f.at[z], ag_r.at[s, z, mine], ag_ss.at[z, k], ag_rs.at[s, z, mine],
+                {"docs": lax.rem(d + k, nd), "sub": core},
+            )
+            if k == 0:
+                pl.when(core != s)(copy.start)
+            else:
+                copy.start()
+            ag_sends.append((copy, k))
+        if z == 0:
             w2_pair.wait_recv()
             w2_sum[1] = w2_sum[0] + w2_in[...]
             w2_z[d] = w2_sum[1]
@@ -360,37 +415,6 @@
                 )
                 copy.start()
                 w2z_sends.append(copy)
-
-    phase("emb_grad")
-    grad = lax.dot_general(
-        pg[0], w1_v[:, :half], (((1,), (1,)), ((), ())), preferred_element_type=F32
-    ) + lax.dot_general(pg[1], w1_v[:, half:], (((1,), (1,)), ((), ())), preferred_element_type=F32)
-    eg_v[...] = grad.astype(BF16)
-    phase("docs_sum")
-    part = nd // 2
-    core = d // part
-    mine = lax.rem(d, part)
-    ag_sends = []
-    for z in range(2):
-        for k in by_distance(nd):
-            src = lax.rem(d + k, nd)
-            remote(z_s.at[0, 0], z_r.at[z, src], z_ss.at[z, k], z_rs.at[z, src], {"docs": src}).wait_recv()
-        z_f[z] = functools.reduce(lambda a, b: a + b, [z_r[z, i].astype(F32) for i in range(nd)]).astype(BF16)
-
-        @pl.when(core == s)
-        def _():
-            ag_r[s, z, mine] = z_f[z]
-
-        for k in by_distance(nd) + [0]:
-            copy = remote(
-                z_f.at[z], ag_r.at[s, z, mine], ag_ss.at[z, k], ag_rs.at[s, z, mine],
-                {"docs": lax.rem(d + k, nd), "sub": core},
-            )
-            if k == 0:
-                pl.when(core != s)(copy.start)
-            else:
-                copy.start()
-            ag_sends.append((copy, k))
 
     phase("w2_z")
     for k in by_distance(nd):
@@ -412,7 +436,7 @@
                 ].astype(F32)
 
     phase("drain")
-    for copy in score_sends + meta_sends + [emb_send, pg_send, w2_pair] + x_sends + w2x_sends + w2z_sends:
+    for copy in score_sends + meta_sends + score_relays + meta_relays + [emb_send, pg_send, w2_pair] + x_sends + w2x_sends + w2z_sends:
         copy.wait_send()
     for copy, to, par in z_sends:
         pl.when(lax.rem(to, 2) == par)(copy.wait_send)
@@ -462,7 +486,6 @@
             pltpu.VMEM((cap, nd, slots), F32),
             pltpu.VMEM((cap, nd, slots), F32),
             pltpu.VMEM((cap, nd, slots), F32),
-            pltpu.VMEM((nd, slots), F32),
             pltpu.VMEM((rows, width), BF16),
             pltpu.VMEM((nm, width // nm, 2 * rows), BF16),
             pltpu.VMEM((2, rows, half), BF16),

time: 98.1 us -> 97 us (0.989)
  Pallas kernels: 97.4 us -> 96.3 us
    pallas_call x1, Pallas kernels: 96.5 us -> 95.4 us  [on_device(): pl.pallas_call(functools.partial(step_kernel, nd, nm, rows, width, cap),...]
where the time goes in v3:
time: 97 us; the launch traced here: 96.9 us
  Pallas kernels  96.3 us (99%)
    pallas_call x1, Pallas kernels, on_device(): pl.pallas_call(functools.partial(step_kernel, nd, nm, rows, width, cap),...  95.4 us

profile of v3, /device:TPU:65, one launch (start us, length us, event | category | flops | bytes accessed | tf_op | source)
XLA Modules:
  0.0 96.9 jit_solution(213969796196966110)
XLA Ops:
  0.6 95.4 %ranking_step.1 = (bf16[128,1024]{1,0:T(8,128)(2,1)S(1)}, f32[64,1024]{1,0:T(8,128)S(1)}, f32[8,128]{1,0:T(8,128)S(1)}) custom-call(bf16[128,1024]{1,0:T(8,128)(2,1)} %emb_h.1, s32[1,128]{1,0:T(1,128)} %bitcast.6, s32[1,128]{1,0:T(1,128)} %bitcast.7, s32[1,128]{1,0:T(1,128)} %bitcast.8, bf16[1024,1024]{1,0:T(8,128)(2,1)} %w1_h.1, f32[1,1024]{1,0:T(1,128)} %bitcast.5), custom_call_target="tpu_custom_call" | custom-call | tf_op jit(solution)/shard_map/ranking_step/pallas_call | solution.py:528
  96.1 0.8 write_out.1

commit v4 on v3

--- a/solution.py
+++ b/solution.py
@@ -143,14 +143,9 @@
         ]
 
 
-    phase("barrier")
-    pl.semaphore_wait(barrier, len(near) + 3)
-    meta_sends = to_near(meta_s, meta_r, meta_ss, meta_rs)
     phase("scorer")
     for copy in loads[3:]:
         copy.wait()
-    emb_send = remote(emb_v, embp_v, pair_ss.at[0], pair_rs.at[0], {"sub": other})
-    emb_send.start()
     score = jnp.zeros((rows, 1), F32)
     for i in range(FWD):
         w_loads[i].wait()
@@ -165,12 +160,24 @@
     score_own = slotted(0.5 * score)
     score_s[...] = score_own
     score_r[0] = score_own
+    phase("barrier")
+    pl.semaphore_wait(barrier, len(near) + 3)
     phase("send_scores")
+    meta_sends = to_near(meta_s, meta_r, meta_ss, meta_rs)
     score_sends = to_near(score_s, score_r, score_ss, score_rs)
+    emb_send = remote(emb_v, embp_v, pair_ss.at[0], pair_rs.at[0], {"sub": other})
+    emb_send.start()
+    phase("near_meta")
     from_near(meta_s, meta_r, meta_ss, meta_rs)
     meta_relays = relays(meta_r, meta_ss, meta_rs)
     for copy in meta_relays:
         copy.start()
+    phase("near_wait")
+    from_near(score_s, score_r, score_ss, score_rs)
+    score_relays = relays(score_r, score_ss, score_rs)
+    for copy in score_relays:
+        copy.start()
+
     phase("turn")
     def turn(block, at):
         for c in range(nm):
@@ -183,12 +190,6 @@
     emb_send.wait_recv()
     turn(embp_v, 1)
 
-    phase("near_wait")
-    from_near(score_s, score_r, score_ss, score_rs)
-    score_relays = relays(score_r, score_ss, score_rs)
-    for copy in score_relays:
-        copy.start()
-
     phase("meta_wait")
     for copy in meta_relays:
         copy.wait_recv()
@@ -206,10 +207,12 @@
     gain = jnp.exp2(label) - 1.0
     sm[0] = mark
     sg[0] = gain
-
+    packed = 32.0 * mark + gain
     for by in range(1, cap):
-        sm[by] = turned(mark, by)
-        sg[by] = turned(gain, by)
+        moved = turned(packed, by)
+        moved_mark = jnp.floor(moved * (1.0 / 32.0))
+        sm[by] = moved_mark
+        sg[by] = moved - 32.0 * moved_mark
 
     group_r = lax.broadcasted_iota(jnp.int32, (slots, slots), 0) // cap
     group_c = lax.broadcasted_iota(jnp.int32, (slots, slots), 1) // cap
@@ -225,12 +228,12 @@
     total = jnp.where(mark == 1.0, counts[0:1], counts[5:6])
     at_least = jnp.where(mark_own == 1.0, counts[1:5], counts[6:10])
 
-    def rank_weight(r, acc):
-        r = r.astype(F32)
-        w = LN2 / jnp.log(jnp.full((4, slots), 2.0, F32) + r)
-        return acc + jnp.where(at_least > r, w, 0.0)
-
-    ladder = lax.fori_loop(0, slots, rank_weight, jnp.zeros((4, slots), F32), unroll=8)
+    at_least = jnp.concatenate([at_least[:, : slots // 2], at_least[:, slots // 2 :]], axis=0)
+    ladders = [jnp.zeros_like(at_least)] * 4
+    for r in range(slots):
+        ladders[r % 4] = ladders[r % 4] + jnp.where(at_least > float(r), 1.0 / math.log2(2.0 + r), 0.0)
+    ladder = (ladders[0] + ladders[1]) + (ladders[2] + ladders[3])
+    ladder = jnp.concatenate([ladder[:4], ladder[4:]], axis=1)
     idcg = ladder[0:1] + 2.0 * ladder[1:2] + 4.0 * ladder[2:3] + 8.0 * ladder[3:4]
     inv = jnp.where(idcg > 0.0, 1.0 / jnp.where(idcg > 0.0, idcg, 1.0), 0.0)
     gain_own = jnp.exp2(label_own) - 1.0
@@ -332,15 +335,19 @@
     product(0)
 
     phase("ring")
-    order = list(range(NQ))
-    for q in order:
-        for side in range(2):
-            if long_way(side, q):
-                ring_send(side, 1, q, ring_recv(side, 0, q) + own(rel_of(side, 1), q))
+    longs = [[q for q in range(NQ) if long_way(side, q)] for side in range(2)]
+    shorts = [[q for q in range(NQ) if not long_way(side, q)] for side in range(2)]
+
+    def forward(step, pieces):
+        for pair in zip(*pieces):
+            for side, q in enumerate(pair):
+                ring_send(side, step, q, ring_recv(side, step - 1, q) + own(rel_of(side, step), q))
+
+    forward(1, longs)
     for step in range(2, far):
-        for q in order:
-            for side in range(2):
-                ring_send(side, step, q, ring_recv(side, step - 1, q) + own(rel_of(side, step), q))
+        forward(step, shorts)
+        forward(step, longs)
+    order = [q for pair in zip(*longs) for q in pair]
 
     phase("ring_end")
     z_sends = []

time: 97 us -> 96.6 us (level)
  no operation moved by 1% of the time
where the time goes in v4:
time: 96.6 us; the launch traced here: 96.5 us
  Pallas kernels  95.8 us (99%)
    pallas_call x1, Pallas kernels, on_device(): pl.pallas_call(functools.partial(step_kernel, nd, nm, rows, width, cap),...  95 us

profile of v4, /device:TPU:65, one launch (start us, length us, event | category | flops | bytes accessed | tf_op | source)
XLA Modules:
  0.0 96.5 jit_solution(6806780721161789529)
XLA Ops:
  0.6 95.0 %ranking_step.1 = (bf16[128,1024]{1,0:T(8,128)(2,1)S(1)}, f32[64,1024]{1,0:T(8,128)S(1)}, f32[8,128]{1,0:T(8,128)S(1)}) custom-call(bf16[128,1024]{1,0:T(8,128)(2,1)} %emb_h.1, s32[1,128]{1,0:T(1,128)} %bitcast.6, s32[1,128]{1,0:T(1,128)} %bitcast.7, s32[1,128]{1,0:T(1,128)} %bitcast.8, bf16[1024,1024]{1,0:T(8,128)(2,1)} %w1_h.1, f32[1,1024]{1,0:T(1,128)} %bitcast.5), custom_call_target="tpu_custom_call" | custom-call | tf_op jit(solution)/shard_map/ranking_step/pallas_call | solution.py:535
  95.6 0.8 write_out.1

commit v5 on v4

--- a/solution.py
+++ b/solution.py
@@ -14,7 +14,8 @@
 
 NQ = 4
 LN2 = math.log(2.0)
-FWD = 4
+NW = 4
+EMB = 4
 
 
 def remote(src, dst, send_sem, recv_sem, where):
@@ -43,15 +44,15 @@
     nd, nm, rows, width, cap,
     emb_h, own_h, qry_h, lab_h, w1_h, w2_h,
     eg_v, out_v, w2_out,
-    emb_v, own_v, qry_v, lab_v, w1_v, w2_v,
+    emb_v, own_v, qry_v, lab_v, w1_v, w2_v, w2_q,
     slope_v, hid_v, hit_v,
     meta_s, meta_r, score_s, score_r,
     sa, sm, sg, sd,
-    embp_v, emb_t, pg, pg_in, g_v,
+    emb_x, emb_t, pg, slope_x, lam_s, lam_r, g_v,
     x_s, x_r, z_s, z_r, z_f, ag_r,
     w2_own, w2_x, w2_sum, w2_in, w2_z,
     load_sem, meta_ss, meta_rs, score_ss, score_rs,
-    pair_ss, pair_rs, x_ss, x_rs, z_ss, z_rs, ag_ss, ag_rs,
+    pair_ss, pair_rs, emb_ss, emb_rs, lam_ss, lam_rs, x_ss, x_rs, z_ss, z_rs, ag_ss, ag_rs,
     w2x_ss, w2x_rs, w2z_ss, w2z_rs,
 ):
     d = lax.axis_index("docs")
@@ -59,8 +60,12 @@
     s = lax.axis_index("sub")
     other = 1 - s
     slots = nd * cap
-    half = width // 2
-    piece = half // NQ
+    quarter = width // NW
+    block_rows = width // nm
+    tiles = block_rows // 16
+    par = lax.rem(d, 2)
+    pair = d + 1 - 2 * par
+    mine_q = 2 * s + par
 
     phase = Phases()
     phase("greet")
@@ -70,12 +75,9 @@
             ((own_h, own_v), (qry_h, qry_v), (lab_h, lab_v), (w2_h, w2_v), (emb_h, emb_v))
         )
     ]
-    cols = width // FWD
     w_loads = [
-        pltpu.make_async_copy(
-            w1_h.at[:, pl.ds(i * cols, cols)], w1_v.at[:, pl.ds(i * cols, cols)], load_sem.at[5 + i]
-        )
-        for i in range(FWD)
+        pltpu.make_async_copy(w1_h.at[:, pl.ds(i * quarter, quarter)], w1_v.at[i], load_sem.at[5 + i])
+        for i in range(NW)
     ]
     for copy in loads + w_loads:
         copy.start()
@@ -88,6 +90,7 @@
     for k in (1, nm - 1):
         pl.semaphore_signal(barrier, inc=1, device_id={"mp": lax.rem(m + k, nm)}, device_id_type=MESH)
     pl.semaphore_signal(barrier, inc=1, device_id={"sub": other}, device_id_type=MESH)
+    pl.semaphore_signal(barrier, inc=1, device_id={"docs": pair, "sub": other}, device_id_type=MESH)
 
     phase("own_slots")
     for copy in loads[:3]:
@@ -144,29 +147,39 @@
 
 
     phase("scorer")
-    for copy in loads[3:]:
+    for copy in loads[3:] + w_loads:
         copy.wait()
-    score = jnp.zeros((rows, 1), F32)
-    for i in range(FWD):
-        w_loads[i].wait()
-        at = pl.ds(i * cols, cols)
-        pre = jnp.dot(emb_v[...], w1_v[:, at], preferred_element_type=F32)
+    terms = jnp.zeros((rows, quarter), F32)
+    for i in range(NW):
+        at = pl.ds(i * quarter, quarter)
+        pre = jnp.dot(emb_v[...], w1_v[i], preferred_element_type=F32)
         sig = 0.5 + 0.5 * jnp.tanh(0.5 * pre)
         hid = pre * sig
-        w2 = w2_v[:, at]
         hid_v[:, at] = hid
-        score += jnp.sum(hid * w2, axis=1, keepdims=True)
-        slope_v[:, at] = w2 * (sig * (1.0 + pre * (1.0 - sig)))
+        slope_v[:, at] = sig
+        w2_q[i] = w2_v[:, at]
+        terms += hid * w2_v[:, at]
+    score = jnp.sum(terms, axis=1, keepdims=True)
     score_own = slotted(0.5 * score)
     score_s[...] = score_own
     score_r[0] = score_own
     phase("barrier")
-    pl.semaphore_wait(barrier, len(near) + 3)
+    pl.semaphore_wait(barrier, len(near) + 4)
     phase("send_scores")
     meta_sends = to_near(meta_s, meta_r, meta_ss, meta_rs)
     score_sends = to_near(score_s, score_r, score_ss, score_rs)
-    emb_send = remote(emb_v, embp_v, pair_ss.at[0], pair_rs.at[0], {"sub": other})
+    emb_send = remote(emb_v, emb_x.at[0], pair_ss.at[0], pair_rs.at[0], {"sub": other})
     emb_send.start()
+    share = rows // EMB
+    emb_moves = [
+        remote(
+            emb_v.at[pl.ds(i * share, share)], emb_x.at[1, pl.ds(i * share, share)],
+            emb_ss.at[i], emb_rs.at[i], {"docs": pair},
+        )
+        for i in range(EMB)
+    ]
+    for copy in emb_moves[:-1]:
+        copy.start()
     phase("near_meta")
     from_near(meta_s, meta_r, meta_ss, meta_rs)
     meta_relays = relays(meta_r, meta_ss, meta_rs)
@@ -178,21 +191,37 @@
     for copy in score_relays:
         copy.start()
 
+    emb_moves[-1].start()
+
     phase("turn")
     def turn(block, at):
         for c in range(nm):
-            w = width // nm
             emb_t[c, :, at * rows : (at + 1) * rows] = (
-                block[:, c * w : (c + 1) * w].astype(F32).T.astype(BF16)
+                block[:, c * block_rows : (c + 1) * block_rows].astype(F32).T.astype(BF16)
             )
 
+    def slope_of(i):
+        pre = jnp.dot(emb_x[i], w1_v[mine_q], preferred_element_type=F32)
+        sig = 0.5 + 0.5 * jnp.tanh(0.5 * pre)
+        slope_x[i] = w2_q[mine_q] * (sig + pre * sig * (1.0 - sig))
+
     turn(emb_v, 0)
+    for i in range(NW):
+        at = pl.ds(i * quarter, quarter)
+        sig = slope_v[:, at]
+        slope_v[:, at] = w2_v[:, at] * (sig + hid_v[:, at] * (1.0 - sig))
     emb_send.wait_recv()
-    turn(embp_v, 1)
+    turn(emb_x.at[0], 1)
+    slope_of(0)
 
     phase("meta_wait")
     for copy in meta_relays:
         copy.wait_recv()
+    phase("emb_wait")
+    for copy in emb_moves:
+        copy.wait_recv()
+    emb_pass = remote(emb_x.at[1], emb_x.at[2], pair_ss.at[1], pair_rs.at[1], {"sub": other})
+    emb_pass.start()
     phase("meta_work")
     lane = lax.broadcasted_iota(jnp.int32, (nd, slots), 1)
     in_group = lax.rem(lane, cap)
@@ -273,16 +302,29 @@
     lam = jnp.sum(jnp.where(hit_v[...] > 0.0, lam_row, 0.0), axis=1, keepdims=True)
 
     phase("pre_grad")
-    for h in range(2):
-        pg[h] = (lam * slope_v[:, h * half : (h + 1) * half]).astype(BF16)
-    pg_send = remote(pg.at[other], pg_in, pair_ss.at[1], pair_rs.at[1], {"sub": other})
-    pg_send.start()
+    lam_s[...] = jnp.sum(jnp.where(eye, lam, 0.0), axis=0, keepdims=True)
+    quad = ({"sub": other}, {"docs": pair}, {"docs": pair, "sub": other})
+    lam_sends = [remote(lam_s, lam_r.at[i], lam_ss.at[i], lam_rs.at[i], where) for i, where in enumerate(quad)]
+    for copy in reversed(lam_sends):
+        copy.start()
+    for i in range(NW):
+        pg[i] = (lam * slope_v[:, i * quarter : (i + 1) * quarter]).astype(BF16)
+    turn(emb_x.at[1], 2)
+    slope_of(1)
     for i in range(width // 128):
         w2_own[i : i + 1, :] = jnp.sum(lam * hid_v[:, i * 128 : (i + 1) * 128], axis=0, keepdims=True)
     w2_x[m] = w2_own[...]
+    phase("emb_pass_wait")
+    emb_pass.wait_recv()
+    turn(emb_x.at[2], 3)
+    slope_of(2)
     phase("pair_wait")
-    pg_send.wait_recv()
-    both = jnp.concatenate([pg[s], pg_in[...]], axis=0)
+    for copy in lam_sends:
+        copy.wait_recv()
+    phase("products")
+    both = jnp.concatenate(
+        [pg[mine_q]] + [(upright(lam_r[i]) * slope_x[i]).astype(BF16) for i in range(3)], axis=0
+    )
 
     right, left = {"mp": lax.rem(m + 1, nm)}, {"mp": lax.rem(m + nm - 1, nm)}
     far = nm // 2
@@ -309,7 +351,8 @@
         return x_r[side, step, q].astype(F32)
 
     def own(rel, q):
-        return g_v[rel, :, q * piece : (q + 1) * piece]
+        lanes = slice((q % 2) * 128, (q % 2) * 128 + 128)
+        return jnp.stack([g_v[rel, e * 16 : e * 16 + 16, lanes] for e in range(q // 2, tiles, 2)])
 
     def rel_of(side, step):
         away = far - step
@@ -318,7 +361,6 @@
     def long_way(side, q):
         return (q < NQ // 2) == (side == 0)
 
-    phase("products")
     product(far)
     for side in range(2):
         for q in range(NQ):
@@ -351,22 +393,26 @@
 
     phase("ring_end")
     z_sends = []
+    planes = nd // 2
+    plane = d // 2
     for q in order:
         block = own(0, q)
         for side in range(2):
             block = block + ring_recv(side, far - 1, q)
-        z_s[q] = block.reshape(nd // 2, 16, piece).astype(BF16)
-        z, par = q // 2, q % 2
-
-        @pl.when(lax.rem(d, 2) == par)
+        z_s[q] = block.astype(BF16)
+        group, z = q // 2, q % 2
+
+        @pl.when(lax.rem(plane, 2) == group)
         def _():
-            z_r[z, d] = z_s[q, d // 2]
-
-        for k in by_distance(nd):
-            to = lax.rem(d + k, nd)
-            copy = remote(z_s.at[q, to // 2], z_r.at[z, d], z_ss.at[z, k], z_rs.at[z, d], {"docs": to})
-            z_sends.append((copy, to, par))
-            pl.when(lax.rem(to, 2) == par)(copy.start)
+            z_r[z, plane] = z_s[q, plane // 2]
+
+        for k in by_distance(planes):
+            to = lax.rem(plane + k, planes)
+            copy = remote(
+                z_s.at[q, to // 2], z_r.at[z, plane], z_ss.at[z, k], z_rs.at[z, plane], {"docs": 2 * to + par}
+            )
+            z_sends.append((copy, to, group))
+            pl.when(lax.rem(to, 2) == group)(copy.start)
 
     w2x_sends = []
     for k in by_distance(nm):
@@ -375,9 +421,13 @@
         w2x_sends.append(copy)
 
     phase("emb_grad")
-    grad = lax.dot_general(
-        pg[0], w1_v[:, :half], (((1,), (1,)), ((), ())), preferred_element_type=F32
-    ) + lax.dot_general(pg[1], w1_v[:, half:], (((1,), (1,)), ((), ())), preferred_element_type=F32)
+    grad = functools.reduce(
+        lambda a, b: a + b,
+        [
+            lax.dot_general(pg[i], w1_v[i], (((1,), (1,)), ((), ())), preferred_element_type=F32)
+            for i in range(NW)
+        ],
+    )
     eg_v[...] = grad.astype(BF16)
     phase("docs_sum")
     for k in by_distance(nm):
@@ -387,23 +437,25 @@
     w2_pair = remote(w2_sum.at[0], w2_in, pair_ss.at[2], pair_rs.at[2], {"sub": other})
     w2_pair.start()
 
-    part = nd // 2
-    core = d // part
-    mine = lax.rem(d, part)
+    part = planes // 2
+    core = plane // part
+    mine = lax.rem(plane, part)
     ag_sends = []
     for z in range(2):
-        for k in by_distance(nd):
-            src = lax.rem(d + k, nd)
-            remote(z_s.at[0, 0], z_r.at[z, src], z_ss.at[z, k], z_rs.at[z, src], {"docs": src}).wait_recv()
-        z_f[z] = functools.reduce(lambda a, b: a + b, [z_r[z, i].astype(F32) for i in range(nd)]).astype(BF16)
+        for k in by_distance(planes):
+            src = lax.rem(plane + k, planes)
+            remote(
+                z_s.at[0, 0], z_r.at[z, src], z_ss.at[z, k], z_rs.at[z, src], {"docs": 2 * src + par}
+            ).wait_recv()
+        z_f[z] = functools.reduce(lambda a, b: a + b, [z_r[z, i].astype(F32) for i in range(planes)]).astype(BF16)
 
         @pl.when(core == s)
         def _():
-            ag_r[s, z, mine] = z_f[z]
+            ag_r[s, par, z, mine] = z_f[z]
 
         for k in by_distance(nd) + [0]:
             copy = remote(
-                z_f.at[z], ag_r.at[s, z, mine], ag_ss.at[z, k], ag_rs.at[s, z, mine],
+                z_f.at[z], ag_r.at[s, par, z, mine], ag_ss.at[z, k], ag_rs.at[s, par, z, mine],
                 {"docs": lax.rem(d + k, nd), "sub": core},
             )
             if k == 0:
@@ -431,22 +483,18 @@
 
     phase("docs_gather")
     for z in range(2):
-        for src in range(2):
+        for src in range(NW):
             for k in range(part):
-                copy = remote(
-                    z_f.at[z], ag_r.at[src, z, k], ag_ss.at[z, k], ag_rs.at[src, z, k], {"sub": other}
-                )
-                same = (src == s) & (s * part + k == d)
+                spot = (src // 2, src % 2, z, k)
+                copy = remote(z_f.at[z], ag_r.at[spot], ag_ss.at[z, k], ag_rs.at[spot], {"sub": other})
+                same = (src // 2 == s) & (2 * (s * part + k) + src % 2 == d)
                 pl.when(jnp.logical_not(same))(copy.wait_recv)
-                out_v[(k // 2) * 16 : (k // 2) * 16 + 16, pl.ds(src * half + z * 256 + (k % 2) * 128, 128)] = ag_r[
-                    src, z, k
-                ].astype(F32)
-
+                out_v[k * 16 : k * 16 + 16, pl.ds(src * quarter + z * 128, 128)] = ag_r[spot].astype(F32)
     phase("drain")
-    for copy in score_sends + meta_sends + score_relays + meta_relays + [emb_send, pg_send, w2_pair] + x_sends + w2x_sends + w2z_sends:
+    for copy in score_sends + meta_sends + score_relays + meta_relays + [emb_send, emb_pass, w2_pair] + emb_moves + lam_sends + x_sends + w2x_sends + w2z_sends:
         copy.wait_send()
-    for copy, to, par in z_sends:
-        pl.when(lax.rem(to, 2) == par)(copy.wait_send)
+    for copy, to, group in z_sends:
+        pl.when(lax.rem(to, 2) == group)(copy.wait_send)
     for copy, k in ag_sends:
         if k == 0:
             pl.when(core != s)(copy.wait_send)
@@ -470,8 +518,8 @@
         rows, width = embeddings.shape
         cap = 2 * rows // nd
         slots = nd * cap
-        half = width // 2
-        piece = half // NQ
+        quarter = width // NW
+        tiles = width // nm // 16
         far = nm // 2
         dma = pltpu.SemaphoreType.DMA
         hbm, vmem, anywhere = (pl.BlockSpec(memory_space=a) for a in (pltpu.HBM, pltpu.VMEM, pl.ANY))
@@ -480,8 +528,9 @@
             pltpu.VMEM((1, rows), jnp.int32),
             pltpu.VMEM((1, rows), jnp.int32),
             pltpu.VMEM((1, rows), jnp.int32),
-            pltpu.VMEM((width, width), BF16),
+            pltpu.VMEM((NW, width, quarter), BF16),
             pltpu.VMEM((1, width), F32),
+            pltpu.VMEM((NW, 1, quarter), F32),
             pltpu.VMEM((rows, width), F32),
             pltpu.VMEM((rows, width), F32),
             pltpu.VMEM((rows, slots), F32),
@@ -493,35 +542,41 @@
             pltpu.VMEM((cap, nd, slots), F32),
             pltpu.VMEM((cap, nd, slots), F32),
             pltpu.VMEM((cap, nd, slots), F32),
-            pltpu.VMEM((rows, width), BF16),
-            pltpu.VMEM((nm, width // nm, 2 * rows), BF16),
-            pltpu.VMEM((2, rows, half), BF16),
-            pltpu.VMEM((rows, half), BF16),
-            pltpu.VMEM((nm, width // nm, half), F32),
-            pltpu.VMEM((2, far, NQ, width // nm, piece), BF16),
-            pltpu.VMEM((2, far, NQ, width // nm, piece), BF16),
-            pltpu.VMEM((NQ, nd // 2, 16, piece), BF16),
-            pltpu.VMEM((2, nd, 16, piece), BF16),
-            pltpu.VMEM((2, 16, piece), BF16),
-            pltpu.VMEM((2, 2, nd // 2, 16, piece), BF16),
+            pltpu.VMEM((3, rows, width), BF16),
+            pltpu.VMEM((nm, width // nm, NW * rows), BF16),
+            pltpu.VMEM((NW, rows, quarter), BF16),
+            pltpu.VMEM((3, rows, quarter), F32),
+            pltpu.VMEM((1, rows), F32),
+            pltpu.VMEM((3, 1, rows), F32),
+            pltpu.VMEM((nm, width // nm, quarter), F32),
+            pltpu.VMEM((2, far, NQ, tiles // 2, 16, 128), BF16),
+            pltpu.VMEM((2, far, NQ, tiles // 2, 16, 128), BF16),
+            pltpu.VMEM((NQ, tiles // 2, 16, 128), BF16),
+            pltpu.VMEM((2, nd // 2, 16, 128), BF16),
+            pltpu.VMEM((2, 16, 128), BF16),
+            pltpu.VMEM((2, 2, 2, nd // 4, 16, 128), BF16),
             pltpu.VMEM((width // 128, 128), F32),
             pltpu.VMEM((nm, width // 128, 128), F32),
             pltpu.VMEM((2, width // 128, 128), F32),
             pltpu.VMEM((width // 128, 128), F32),
             pltpu.VMEM((nd, width // 128, 128), F32),
-            dma((5 + FWD,)),
+            dma((5 + NW,)),
             dma((nd,)),
             dma((nd,)),
             dma((nd,)),
             dma((nd,)),
             dma((3,)),
             dma((3,)),
+            dma((EMB,)),
+            dma((EMB,)),
+            dma((3,)),
+            dma((3,)),
             dma((2, far, NQ)),
             dma((2, far, NQ)),
+            dma((2, nd // 2)),
+            dma((2, nd // 2)),
             dma((2, nd)),
-            dma((2, nd)),
-            dma((2, nd)),
-            dma((2, 2, nd // 2)),
+            dma((2, 2, 2, nd // 4)),
             dma((nm,)),
             dma((nm,)),
             dma((nd,)),

time: 96.6 us -> 95.3 us (0.987)
  Pallas kernels: 95.8 us -> 94.5 us
    pallas_call x1, Pallas kernels: 95 us -> 93.6 us  [on_device(): pl.pallas_call(functools.partial(step_kernel, nd, nm, rows, width, cap),...]
where the time goes in v5:
time: 95.3 us; the launch traced here: 95.1 us
  Pallas kernels  94.5 us (99%)
    pallas_call x1, Pallas kernels, on_device(): pl.pallas_call(functools.partial(step_kernel, nd, nm, rows, width, cap),...  93.6 us

profile of v5, /device:TPU:65, one launch (start us, length us, event | category | flops | bytes accessed | tf_op | source)
XLA Modules:
  0.0 95.1 jit_solution(11391556174977713348)
XLA Ops:
  0.6 93.6 %ranking_step.1 = (bf16[128,1024]{1,0:T(8,128)(2,1)S(1)}, f32[64,1024]{1,0:T(8,128)S(1)}, f32[8,128]{1,0:T(8,128)S(1)}) custom-call(bf16[128,1024]{1,0:T(8,128)(2,1)} %emb_h.1, s32[1,128]{1,0:T(1,128)} %bitcast.6, s32[1,128]{1,0:T(1,128)} %bitcast.7, s32[1,128]{1,0:T(1,128)} %bitcast.8, bf16[1024,1024]{1,0:T(8,128)(2,1)} %w1_h.1, f32[1,1024]{1,0:T(1,128)} %bitcast.5), custom_call_target="tpu_custom_call" | custom-call | tf_op jit(solution)/shard_map/ranking_step/pallas_call | solution.py:590
  94.3 0.8 write_out.1

commit v6 on v5

--- a/solution.py
+++ b/solution.py
@@ -87,7 +87,7 @@
     near = [k for k in by_distance(nd) if min(k, nd - k) <= reach]
     for k in near:
         pl.semaphore_signal(barrier, inc=1, device_id={"docs": lax.rem(d + k, nd)}, device_id_type=MESH)
-    for k in (1, nm - 1):
+    for k in (1, 2, nm - 2, nm - 1):
         pl.semaphore_signal(barrier, inc=1, device_id={"mp": lax.rem(m + k, nm)}, device_id_type=MESH)
     pl.semaphore_signal(barrier, inc=1, device_id={"sub": other}, device_id_type=MESH)
     pl.semaphore_signal(barrier, inc=1, device_id={"docs": pair, "sub": other}, device_id_type=MESH)
@@ -164,7 +164,7 @@
     score_s[...] = score_own
     score_r[0] = score_own
     phase("barrier")
-    pl.semaphore_wait(barrier, len(near) + 4)
+    pl.semaphore_wait(barrier, len(near) + 6)
     phase("send_scores")
     meta_sends = to_near(meta_s, meta_r, meta_ss, meta_rs)
     score_sends = to_near(score_s, score_r, score_ss, score_rs)
@@ -313,7 +313,12 @@
     slope_of(1)
     for i in range(width // 128):
         w2_own[i : i + 1, :] = jnp.sum(lam * hid_v[:, i * 128 : (i + 1) * 128], axis=0, keepdims=True)
-    w2_x[m] = w2_own[...]
+    w2_z[d] = w2_own[...]
+    w2z_sends = []
+    for k in by_distance(nd):
+        copy = remote(w2_own, w2_z.at[d], w2z_ss.at[k], w2z_rs.at[d], {"docs": lax.rem(d + k, nd)})
+        copy.start()
+        w2z_sends.append(copy)
     phase("emb_pass_wait")
     emb_pass.wait_recv()
     turn(emb_x.at[2], 3)
@@ -326,8 +331,12 @@
         [pg[mine_q]] + [(upright(lam_r[i]) * slope_x[i]).astype(BF16) for i in range(3)], axis=0
     )
 
-    right, left = {"mp": lax.rem(m + 1, nm)}, {"mp": lax.rem(m + nm - 1, nm)}
     far = nm // 2
+
+    def hop(side, step):
+        hops = 2 if step == 0 else 1
+        return {"mp": lax.rem(m + (hops if side == 0 else nm - hops), nm)}
+
 
     def product(rel):
         g_v[rel] = jnp.dot(emb_t[lax.rem(m + rel, nm)], both, preferred_element_type=F32)
@@ -338,7 +347,7 @@
         x_s[side, step, q] = value.astype(BF16)
         copy = remote(
             x_s.at[side, step, q], x_r.at[side, step, q], x_ss.at[side, step, q], x_rs.at[side, step, q],
-            (right, left)[side],
+            hop(side, step),
         )
         copy.start()
         x_sends.append(copy)
@@ -346,7 +355,7 @@
     def ring_recv(side, step, q):
         remote(
             x_s.at[side, step, q], x_r.at[side, step, q], x_ss.at[side, step, q], x_rs.at[side, step, q],
-            (right, left)[side],
+            hop(side, step),
         ).wait_recv()
         return x_r[side, step, q].astype(F32)
 
@@ -361,31 +370,31 @@
     def long_way(side, q):
         return (q < NQ // 2) == (side == 0)
 
+    longs = [[q for q in range(NQ) if long_way(side, q)] for side in range(2)]
+    shorts = [[q for q in range(NQ) if not long_way(side, q)] for side in range(2)]
     product(far)
     for side in range(2):
-        for q in range(NQ):
-            if long_way(side, q):
-                ring_send(side, 0, q, own(far, q))
+        for q in longs[side]:
+            ring_send(side, 0, q, own(far, q))
     for side in range(2):
         product(rel_of(side, 1))
-        for q in range(NQ):
-            if not long_way(side, q):
-                ring_send(side, 1, q, own(rel_of(side, 1), q))
+        for q in shorts[side] + longs[side]:
+            ring_send(side, 1, q, own(rel_of(side, 1), q))
     for step in range(2, far):
         for side in range(2):
             product(rel_of(side, step))
     product(0)
 
     phase("ring")
-    longs = [[q for q in range(NQ) if long_way(side, q)] for side in range(2)]
-    shorts = [[q for q in range(NQ) if not long_way(side, q)] for side in range(2)]
 
     def forward(step, pieces):
         for pair in zip(*pieces):
             for side, q in enumerate(pair):
-                ring_send(side, step, q, ring_recv(side, step - 1, q) + own(rel_of(side, step), q))
-
-    forward(1, longs)
+                block = ring_recv(side, step - 1, q) + own(rel_of(side, step), q)
+                if step == 2 and q in longs[side]:
+                    block = block + ring_recv(side, 0, q)
+                ring_send(side, step, q, block)
+
     for step in range(2, far):
         forward(step, shorts)
         forward(step, longs)
@@ -414,9 +423,14 @@
             z_sends.append((copy, to, group))
             pl.when(lax.rem(to, 2) == group)(copy.start)
 
+    for k in by_distance(nd):
+        src = lax.rem(d + k, nd)
+        remote(w2_own, w2_z.at[src], w2z_ss.at[k], w2z_rs.at[src], {"docs": src}).wait_recv()
+    w2_sum[0] = functools.reduce(lambda a, b: a + b, [w2_z[i] for i in range(nd)])
+    w2_x[m] = w2_sum[0]
     w2x_sends = []
     for k in by_distance(nm):
-        copy = remote(w2_own, w2_x.at[m], w2x_ss.at[k], w2x_rs.at[m], {"mp": lax.rem(m + k, nm)})
+        copy = remote(w2_sum.at[0], w2_x.at[m], w2x_ss.at[k], w2x_rs.at[m], {"mp": lax.rem(m + k, nm)})
         copy.start()
         w2x_sends.append(copy)
 
@@ -430,13 +444,6 @@
     )
     eg_v[...] = grad.astype(BF16)
     phase("docs_sum")
-    for k in by_distance(nm):
-        src = lax.rem(m + k, nm)
-        remote(w2_own, w2_x.at[src], w2x_ss.at[k], w2x_rs.at[src], {"mp": src}).wait_recv()
-    w2_sum[0] = functools.reduce(lambda a, b: a + b, [w2_x[i] for i in range(nm)])
-    w2_pair = remote(w2_sum.at[0], w2_in, pair_ss.at[2], pair_rs.at[2], {"sub": other})
-    w2_pair.start()
-
     part = planes // 2
     core = plane // part
     mine = lax.rem(plane, part)
@@ -464,22 +471,15 @@
                 copy.start()
             ag_sends.append((copy, k))
         if z == 0:
-            w2_pair.wait_recv()
-            w2_sum[1] = w2_sum[0] + w2_in[...]
-            w2_z[d] = w2_sum[1]
-            w2z_sends = []
-            for k in by_distance(nd):
-                copy = remote(
-                    w2_sum.at[1], w2_z.at[d], w2z_ss.at[k], w2z_rs.at[d], {"docs": lax.rem(d + k, nd)}
-                )
-                copy.start()
-                w2z_sends.append(copy)
-
-    phase("w2_z")
-    for k in by_distance(nd):
-        src = lax.rem(d + k, nd)
-        remote(w2_sum.at[1], w2_z.at[src], w2z_ss.at[k], w2z_rs.at[src], {"docs": src}).wait_recv()
-    w2_out[...] = functools.reduce(lambda a, b: a + b, [w2_z[i] for i in range(nd)])
+            for k in by_distance(nm):
+                src = lax.rem(m + k, nm)
+                remote(w2_sum.at[0], w2_x.at[src], w2x_ss.at[k], w2x_rs.at[src], {"mp": src}).wait_recv()
+            w2_sum[1] = functools.reduce(lambda a, b: a + b, [w2_x[i] for i in range(nm)])
+            w2_pair = remote(w2_sum.at[1], w2_in, pair_ss.at[2], pair_rs.at[2], {"sub": other})
+            w2_pair.start()
+
+    w2_pair.wait_recv()
+    w2_out[...] = w2_sum[1] + w2_in[...]
 
     phase("docs_gather")
     for z in range(2):

time: 95.3 us -> 92 us (0.965)
  Pallas kernels: 94.5 us -> 91.2 us
    pallas_call x1, Pallas kernels: 93.6 us -> 90.4 us  [on_device(): pl.pallas_call(functools.partial(step_kernel, nd, nm, rows, width, cap),...]
where the time goes in v6:
time: 92 us; the launch traced here: 91.8 us
  Pallas kernels  91.2 us (99%)
    pallas_call x1, Pallas kernels, on_device(): pl.pallas_call(functools.partial(step_kernel, nd, nm, rows, width, cap),...  90.4 us

profile of v6, /device:TPU:65, one launch (start us, length us, event | category | flops | bytes accessed | tf_op | source)
XLA Modules:
  0.0 91.8 jit_solution(15914803526584904743)
XLA Ops:
  0.6 90.4 %ranking_step.1 = (bf16[128,1024]{1,0:T(8,128)(2,1)S(1)}, f32[64,1024]{1,0:T(8,128)S(1)}, f32[8,128]{1,0:T(8,128)S(1)}) custom-call(bf16[128,1024]{1,0:T(8,128)(2,1)} %emb_h.1, s32[1,128]{1,0:T(1,128)} %bitcast.6, s32[1,128]{1,0:T(1,128)} %bitcast.7, s32[1,128]{1,0:T(1,128)} %bitcast.8, bf16[1024,1024]{1,0:T(8,128)(2,1)} %w1_h.1, f32[1,1024]{1,0:T(1,128)} %bitcast.5), custom_call_target="tpu_custom_call" | custom-call | tf_op jit(solution)/shard_map/ranking_step/pallas_call | solution.py:590
  91.0 0.8 write_out.1
